TPU v7x, 128 devices: a whole 4x4x4 slice. The times are simulated.
128 devices in a mesh: inst: 8 (over y_hi, x), head: 16 (over y_lo, z, core).
Axes of the slice: x: 4, y: 4 (y_hi: 2, y_lo: 2; y = y_hi * 2 + y_lo), z: 4, core: 2. Of those that a mesh axis runs over, the one named last changes fastest.
Arguments:
- old_keys: bfloat16 [1024, 16, 64, 128], P('inst', 'head'), may hold values from -6 to 6
- old_values: bfloat16 [1024, 16, 64, 128], P('inst', 'head'), may hold values from -6 to 6
- old_block: int32 [1024], P('inst'), may hold values from -1 to 255, as said below
- new_slot: int32 [256], replicated, may hold values from 0 to 255, as said below
- lengths: int32 [64], replicated, may hold values from 1 to 16384, as said below
- queries: bfloat16 [64, 16, 8192], P(None, None, 'head'), may hold values from -240 to 240
- draft_keys: bfloat16 [64, 16, 1024], P('inst'), may hold values from -6 to 6
- draft_values: bfloat16 [64, 16, 1024], P('inst'), may hold values from -6 to 6
Outputs:
- moved_keys: bfloat16 [256, 16, 64, 128], P('inst', 'head')
- moved_values: bfloat16 [256, 16, 64, 128], P('inst', 'head')
- attended: bfloat16 [64, 16, 8192], P(None, None, 'head')
Inputs may be any that keep to these rules, and one draw needn't show every extreme that they name: ceil(lengths / 128) summed over the requests is exactly 256; the longest request has exactly 16384 tokens. `old_block`: every block 0 to 255 stands in exactly one old slot; the blocks fill all slots of 2 instances and all other slots hold -1. A permutation; block g goes to instance new_slot[g] // 32. At most 32 blocks go from one old instance to one new one, and in every draw some new instance receives all its 32 blocks from a single old instance.
All inputs are finite; a program needn't handle non-finite values.
Results may differ from a plain program's by a relative error of at most 0.004.
Values may be sent and summed in bfloat16 or wider, within the bound.
No kernel may reach another device: no remote copies, remote signals or barrier semaphores. Data moves between devices by JAX's collectives and lax.ppermute only.
A program may use at most 64 MiB of HBM per device.

v0:
```python
import functools
import math

import jax
import jax.numpy as jnp
from jax import lax
from jax.experimental import pallas as pl
from jax.experimental.pallas import tpu as pltpu
from jax.sharding import PartitionSpec as P


BLK = 128
masked = -1e30


COLS = 4
SENT_K = ((4, 3), (5, 6))
SENT_V = ((5,), (3, 7))
KEPT_K = ((2,), (7,), (0,), (1,))
KEPT_V = ((1,), (4,), (2,), (6,), (0,))


def pack_body(groups_k, groups_v, old_block, new_slot, base, keys, values, *rest):
    count = len(groups_k) + len(groups_v)
    outs = rest[:count]
    vk, vv, zeros, origin, sems, load_sem = rest[count:]
    slots = keys.shape[0]
    total = new_slot.shape[0]
    per = zeros.shape[0]
    is_source = old_block[0] >= 0
    jobs = [(vk, out, group) for out, group in zip(outs, groups_k)]
    jobs += [(vv, out, group) for out, group in zip(outs[len(groups_k) :], groups_v)]

    @pl.when(is_source)
    def _():
        load_k = pltpu.make_async_copy(keys, vk, load_sem.at[0])
        load_v = pltpu.make_async_copy(values, vv, load_sem.at[1])
        load_k.start()
        load_v.start()
        zeros[0] = jnp.zeros(zeros.shape[1:], zeros.dtype)

        def clear(t, c):
            origin[t] = -1
            return c

        lax.fori_loop(0, total, clear, 0, unroll=8)

        def note(i, c):
            origin[new_slot[jnp.maximum(old_block[i], 0)]] = i
            return c

        lax.fori_loop(0, slots, note, 0, unroll=8)
        load_k.wait()
        load_v.wait()
        for at, (cache, out, group) in enumerate(jobs):
            for g, p in enumerate(group):
                start = base[p]

                def send(j, c, cache=cache, out=out, at=at, g=g, start=start):
                    i = origin[start + j]

                    @pl.when(i >= 0)
                    def _():
                        pltpu.make_async_copy(cache.at[i], out.at[g * per + j], sems.at[at]).start()

                    @pl.when(i < 0)
                    def _():
                        pltpu.make_async_copy(zeros.at[0], out.at[g * per + j], sems.at[at]).start()

                    return c

                lax.fori_loop(0, per, send, 0, unroll=4)

    @pl.when(jnp.logical_not(is_source))
    def _():
        zeros[...] = jnp.zeros(zeros.shape, zeros.dtype)
        for at, (cache, out, group) in enumerate(jobs):
            for g in range(len(group)):
                pltpu.make_async_copy(zeros, out.at[pl.ds(g * per, per)], sems.at[at]).start()

    for at, (cache, out, group) in enumerate(jobs):
        pltpu.make_async_copy(out, out, sems.at[at]).wait()


def table_of(per, rows, half, head_dim):
    insts = lax.axis_size("inst")
    inst = lax.axis_index("inst")
    me_head = lax.axis_index("head")
    step = jnp.arange(16, dtype=jnp.int32)
    away = (inst // COLS) ^ (step % 2)
    column = (inst % COLS + step // 2) % COLS
    base = (away * COLS + column) * per
    rest = jnp.where(
        step == insts,
        inst * rows,
        jnp.where(step == insts + 1, me_head % 2 * half, me_head // 2 * head_dim),
    )
    return jnp.where(step < insts, base, rest)


def pack(old_block, new_slot, base, keys, values, insts, groups_k, groups_v):
    total = new_slot.shape[0]
    per = total // insts
    groups = groups_k + groups_v
    anyspace = pl.BlockSpec(memory_space=pl.ANY)
    smem = pl.BlockSpec(memory_space=pltpu.SMEM)
    got = pl.pallas_call(
        functools.partial(pack_body, groups_k, groups_v),
        in_specs=[smem, smem, smem, anyspace, anyspace],
        out_specs=[anyspace] * len(groups),
        out_shape=[
            jax.ShapeDtypeStruct((per * len(g),) + keys.shape[1:], keys.dtype) for g in groups
        ],
        scratch_shapes=[
            pltpu.VMEM(keys.shape, keys.dtype),
            pltpu.VMEM(keys.shape, keys.dtype),
            pltpu.VMEM((per,) + keys.shape[1:], keys.dtype),
            pltpu.SMEM((total,), jnp.int32),
            pltpu.SemaphoreType.DMA((len(groups),)),
            pltpu.SemaphoreType.DMA((2,)),
        ],
    )(old_block, new_slot, base, keys, values)
    return got[: len(groups_k)], got[len(groups_k) :]


def right(x):
    rows = lax.axis_size("inst") // COLS
    route = [(r * COLS + c, r * COLS + (c + 1) % COLS) for r in range(rows) for c in range(COLS)]
    return lax.ppermute(x, "inst", route)


def left(x):
    rows = lax.axis_size("inst") // COLS
    route = [(r * COLS + (c + 1) % COLS, r * COLS + c) for r in range(rows) for c in range(COLS)]
    return lax.ppermute(x, "inst", route)


def across(x):
    return lax.ppermute(x, "inst", [(i, i ^ COLS) for i in range(lax.axis_size("inst"))])


def move_keys(from_left, from_right, groups):
    k1n, k3f, k0n, k0f = groups
    per = k1n.shape[0]
    a2 = right(k1n + from_left[:per])
    b2 = left(k3f + from_right[:per])
    b2, from_left = lax.optimization_barrier((b2, from_left))
    crossed = across(k0f + from_left[per:] + b2)
    return k0n + from_right[per:] + a2 + crossed


def move_values(got2, got, y0, groups):
    v2n, v1n, v3n, v0n = groups
    per = v1n.shape[0]
    cut = per // 2
    from_left = right(v2n[:cut] + got2[:cut])
    from_right = left(v2n[cut:] + got2[cut:])
    rest = jnp.zeros((per - cut,) + v1n.shape[1:], v1n.dtype)
    a2 = right(v1n + got[:per] + jnp.concatenate([from_left, rest]))
    b2 = left(v3n + got[per:] + jnp.concatenate([rest, from_right]))
    return v0n + y0 + a2 + b2


def dot_t(x, y):
    return lax.dot_general(x, y, (((1,), (1,)), ((), ())), preferred_element_type=jnp.float32)


def attend_body(
    old_block, lengths, meta, q, k, v, ok, ov, dks, dvs, packet,
    vq, dk, dv, vk, vv, vok, vov, scores, drafted, peak, total, acc, owner, live, sems,
):
    requests, draft, width = vq.shape
    head_dim = vk.shape[2]
    half = vk.shape[1]
    slots = vk.shape[0]
    heads = width // head_dim
    qrows = draft * heads
    insts = packet.shape[0]
    rows = requests // insts
    inv_root = 1.0 / math.sqrt(head_dim)
    is_source = old_block[0] >= 0
    first = meta[insts]
    shift = meta[insts + 1]
    kv = pl.ds(pl.multiple_of(meta[insts + 2], head_dim), head_dim)
    early = [
        pltpu.make_async_copy(q, vq, sems.at[0]),
        pltpu.make_async_copy(dks.at[:, :, kv], dk, sems.at[5]),
        pltpu.make_async_copy(dvs.at[:, :, kv], dv, sems.at[6]),
    ]
    for load in early:
        load.start()
    loads = [
        pltpu.make_async_copy(x, y, sems.at[1 + n])
        for n, (x, y) in enumerate(((k, vk), (ok, vok), (v, vv), (ov, vov)))
    ]

    @pl.when(is_source)
    def _():
        for load in loads:
            load.start()

        def per_request(r, g):
            size = lengths[r]

            def per_block(j, c):
                owner[g + j] = r
                live[g + j] = jnp.minimum(size - j * BLK, BLK)
                return c

            n = (size + BLK - 1) // BLK
            lax.fori_loop(0, n, per_block, 0)
            return g + n

        lax.fori_loop(0, requests, per_request, 0)

    def q_of(r):
        return jnp.concatenate(
            [vq[r, :, h * head_dim : (h + 1) * head_dim] for h in range(heads)], axis=0
        )

    lane = lax.broadcasted_iota(jnp.int32, (qrows, head_dim), 1)
    row = lax.broadcasted_iota(jnp.int32, (qrows, head_dim), 0)
    place = (lane + shift) % (2 * half)
    causal = lane <= row % draft
    blank = jnp.full((qrows, head_dim), masked, jnp.float32)

    def reset(r, c):
        peak[r] = blank
        return c

    lax.fori_loop(0, requests, reset, 0, unroll=4)
    for load in early:
        load.wait()
    pad = jnp.zeros((2 * half - draft, head_dim), dk.dtype)
    for a in range(rows):
        s = dot_t(q_of(first + a), jnp.concatenate([dk[a], pad], axis=0)) * inv_root
        s = jnp.where(causal, s, masked)
        drafted[a] = s
        peak[first + a] = s

    @pl.when(is_source)
    def _():
        loads[0].wait()
        loads[1].wait()

        def score(n, c):
            found = []
            for u in range(UNROLL):
                i = n * UNROLL + u
                g = jnp.maximum(old_block[i], 0)
                r = owner[g]
                key = jnp.concatenate([vk[i], vok[i]], axis=0)
                s = dot_t(q_of(r), key) * inv_root
                found.append((i, r, jnp.where(place < live[g], s, masked)))
            for i, r, s in found:
                scores[i] = s
                peak[r] = jnp.maximum(peak[r], s)
            return c

        lax.fori_loop(0, slots // UNROLL, score, 0)

    def settle(r, c):
        peak[r] = jnp.broadcast_to(jnp.max(peak[r], axis=1, keepdims=True), (qrows, head_dim))
        total[r] = jnp.zeros((qrows, head_dim), jnp.float32)
        acc[r] = jnp.zeros((qrows, head_dim), jnp.float32)
        return c

    lax.fori_loop(0, requests, settle, 0, unroll=SETTLE)
    for a in range(rows):
        w = jnp.exp(drafted[a] - peak[first + a])
        total[first + a] = w
        acc[first + a] = jnp.dot(
            w.astype(dv.dtype),
            jnp.concatenate([dv[a], pad], axis=0),
            preferred_element_type=jnp.float32,
        )

    @pl.when(is_source)
    def _():
        loads[2].wait()
        loads[3].wait()

        def gather(n, c):
            found = []
            for u in range(UNROLL):
                i = n * UNROLL + u
                r = owner[jnp.maximum(old_block[i], 0)]
                w = jnp.exp(scores[i] - peak[r])
                value = jnp.concatenate([vv[i], vov[i]], axis=0)
                out = jnp.dot(w.astype(vv.dtype), value, preferred_element_type=jnp.float32)
                found.append((r, w, out))
            for r, w, out in found:
                total[r] += w
                acc[r] += out
            return c

        lax.fori_loop(0, slots // UNROLL, gather, 0)

    def finish(d, c):
        sums = jnp.zeros((qrows, head_dim), jnp.float32)
        tops = jnp.zeros((qrows, head_dim), jnp.float32)
        for a in range(rows):
            r = d * rows + a
            l = jnp.sum(total[r], axis=1, keepdims=True)
            scale = 1.0 / jnp.where(l > 0, l, 1.0)
            packet[d, a * qrows : (a + 1) * qrows, :] = (acc[r] * scale).astype(packet.dtype)
            sums = jnp.where(lane % rows == a, l, sums)
            tops = jnp.where(lane % rows == a, peak[r], tops)
        level = jnp.where(sums > 0, tops + jnp.log(jnp.where(sums > 0, sums, 1.0)), masked)
        hi = level.astype(jnp.bfloat16).astype(jnp.float32)
        mid = (level - hi).astype(jnp.bfloat16).astype(jnp.float32)
        stat = jnp.where(lane < rows, hi, jnp.where(lane < 2 * rows, mid, level - hi - mid))
        packet[d, rows * qrows :, :] = stat.astype(packet.dtype)
        return c

    lax.fori_loop(0, insts, finish, 0)


UNROLL = 16
SETTLE = 16


def attend(old_block, lengths, meta, queries, keys, values, other_k, other_v, dk, dv, insts):
    requests, draft, width = queries.shape
    head_dim = keys.shape[2]
    qrows = draft * width // head_dim
    rows = requests // insts
    anyspace = pl.BlockSpec(memory_space=pl.ANY)
    smem = pl.BlockSpec(memory_space=pltpu.SMEM)
    vmem = pl.BlockSpec(memory_space=pltpu.VMEM)
    bf16 = jnp.bfloat16
    state = pltpu.VMEM((requests, qrows, head_dim), jnp.float32)
    return pl.pallas_call(
        attend_body,
        in_specs=[smem] * 3 + [anyspace] * 7,
        out_specs=vmem,
        out_shape=jax.ShapeDtypeStruct((insts, (rows + 1) * qrows, head_dim), bf16),
        scratch_shapes=[pltpu.VMEM(queries.shape, bf16)]
        + [pltpu.VMEM((rows, draft, head_dim), bf16)] * 2
        + [pltpu.VMEM(keys.shape, bf16)] * 4
        + [
            pltpu.VMEM((keys.shape[0], qrows, head_dim), jnp.float32),
            pltpu.VMEM((rows, qrows, head_dim), jnp.float32),
            state,
            state,
            state,
            pltpu.SMEM((TOTAL,), jnp.int32),
            pltpu.SMEM((TOTAL,), jnp.int32),
            pltpu.SemaphoreType.DMA((7,)),
        ],
        name="attend",
    )(old_block, lengths, meta, queries, keys, values, other_k, other_v, dk, dv)


TOTAL = 256


def join_body(got, out):
    insts, _, head_dim = got.shape
    rows = out.shape[1]
    draft = out.shape[2]
    heads = out.shape[3] // head_dim
    qrows = draft * heads
    lane = lax.broadcasted_iota(jnp.int32, (qrows, head_dim), 1)
    stats = [got[s, rows * qrows :, :].astype(jnp.float32) for s in range(insts)]
    for a in range(rows):
        mine = (lane % rows == a) & (lane < 3 * rows)
        level = [
            jnp.sum(jnp.where(mine, stat, 0.0), axis=1, keepdims=True) for stat in stats
        ]
        top = level[0]
        for x in level[1:]:
            top = jnp.maximum(top, x)
        total = jnp.zeros((qrows, 1), jnp.float32)
        acc = jnp.zeros((qrows, head_dim), jnp.float32)
        for s in range(insts):
            share = jnp.exp(level[s] - top)
            total = total + share
            acc = acc + share * got[s, a * qrows : (a + 1) * qrows, :].astype(jnp.float32)
        res = (acc / total).astype(out.dtype)
        for d in range(insts):
            for h in range(heads):
                out[d, a, :, h * head_dim : (h + 1) * head_dim] = res[h * draft : (h + 1) * draft]


def join(got, rows, draft, width):
    insts = got.shape[0]
    vmem = pl.BlockSpec(memory_space=pltpu.VMEM)
    return pl.pallas_call(
        join_body,
        in_specs=[vmem],
        out_specs=vmem,
        out_shape=jax.ShapeDtypeStruct((insts, rows, draft, width), got.dtype),
        name="join",
    )(got)


def spread(x):
    return lax.all_to_all(x, "inst", split_axis=0, concat_axis=0, tiled=True)


def move_and_attend(
    old_keys, old_values, old_block, new_slot, lengths, queries, draft_keys, draft_values
):
    insts = lax.axis_size("inst")
    _, entries, half, head_dim = old_keys.shape
    keys = old_keys.reshape(-1, half, head_dim)
    values = old_values.reshape(-1, half, head_dim)
    blocks = new_slot.shape[0]
    requests = queries.shape[0]
    rows = requests // insts
    swap = [(i, i ^ 1) for i in range(lax.axis_size("head"))]
    other_k = lax.ppermute(keys, "head", swap)
    other_v = lax.ppermute(values, "head", swap)

    table = table_of(blocks // insts, rows, half, head_dim)
    out_k, out_v = pack(old_block, new_slot, table, keys, values, insts, SENT_K, SENT_V)
    queries, out_k, out_v = lax.optimization_barrier((queries, out_k, out_v))
    shape = (blocks // insts, entries, half, head_dim)
    far2 = across(out_v[0])
    from_left = right(out_k[0])
    from_right = left(out_k[1])
    far = across(out_v[1])
    kept_k, kept_v = pack(old_block, new_slot, table, keys, values, insts, KEPT_K, KEPT_V)
    near = across(kept_v[0])
    packet = attend(
        old_block, lengths, table, queries, keys, values, other_k, other_v,
        draft_keys, draft_values, insts,
    )
    packet, rest_k, rest_v = lax.optimization_barrier((packet, kept_k, kept_v[1:]))
    moved_keys = move_keys(from_left, from_right, rest_k).reshape(shape)
    moved_values = move_values(far2, far, near, rest_v).reshape(shape)
    got = spread(packet)
    mine = join(got, rows, queries.shape[1], queries.shape[2])
    attended = spread(mine).reshape(queries.shape)
    return moved_keys, moved_values, attended


def solution(mesh):
    placed = (
        P("inst", "head", None, None),
        P("inst", "head", None, None),
        P("inst"),
        P(),
        P(),
        P(None, None, "head"),
        P("inst", None, None),
        P("inst", None, None),
    )
    return jax.shard_map(
        move_and_attend,
        mesh=mesh,
        in_specs=placed,
        out_specs=(
            P("inst", "head", None, None),
            P("inst", "head", None, None),
            P(None, None, "head"),
        ),
        check_vma=False,
    )
```

profile of v0, /device:TPU:0, one launch (start us, length us, event | category | flops | bytes accessed | tf_op | source)
XLA Modules:
  0.0 113.0 jit_solution(13982430479264169501)
XLA Ops:
  0.6 0.1 collective-permute-start
  0.7 0.5 collective-permute-start.1
  1.2 0.5 compare_select_fusion.4.base.meta
  1.7 2.6 %shard_map.103 = (bf16[64,64,128]{2,1,0:T(8,128)(2,1)}, bf16[64,64,128]{2,1,0:T(8,128)(2,1)}, bf16[32,64,128]{2,1,0:T(8,128)(2,1)}, bf16[64,64,128]{2,1,0:T(8,128)(2,1)}) custom-call(s32[128]{0:T(128)} %old_block.5, s32[256]{0:T(256)} %new_slot.3, s32[16]{0:T(128)} %compare_select_fusion.4.base.meta, bf16[128,64,128]{2,1,0:T(8,128)(2,1)} %bitcast.12, ...), custom_call_target="tpu_custom_call" | custom-call | tf_op jit(solution)/shard_map/pallas_call | solution.py:107
  4.4 2.9 %collective-permute-start.2 = (bf16[64,64,128]{2,1,0:T(8,128)(2,1)}, bf16[64,64,128]{2,1,0:T(8,128)(2,1)S(1)}, u32[]{:S(2)}, u32[]{:S(2)}) collective-permute-start(bf16[64,64,128]{2,1,0:T(8,128)(2,1)} %get-tuple-element.46), channel_id=1, source_target_pairs={{16,0},{32,16},{48,32},{0,48},{80,64},{96,80},{112,96},{64,112},{1... | collective-permute-start | bytes 3145736 | tf_op jit(solution)/shard_map/ppermute | solution.py:135
  7.3 3.2 %collective-permute-start.8 = (bf16[64,64,128]{2,1,0:T(8,128)(2,1)}, bf16[64,64,128]{2,1,0:T(8,128)(2,1)}, u32[]{:S(2)}, u32[]{:S(2)}) collective-permute-start(bf16[64,64,128]{2,1,0:T(8,128)(2,1)} %get-tuple-element.56), channel_id=1, source_target_pairs={{0,64},{16,80},{32,96},{48,112},{64,0},{80,16},{96,32},{112,48},{1... | collective-permute-start | bytes 3145736 | tf_op jit(solution)/shard_map/ppermute | solution.py:139
  10.5 0.3 collective-permute-start.9
  10.9 0.0 collective-permute-done.ok
  10.9 1.1 collective-permute-start.3
  12.0 3.1 %shard_map.104 = (bf16[32,64,128]{2,1,0:T(8,128)(2,1)}, bf16[32,64,128]{2,1,0:T(8,128)(2,1)}, bf16[32,64,128]{2,1,0:T(8,128)(2,1)}, bf16[32,64,128]{2,1,0:T(8,12...) custom-call(s32[128]{0:T(128)} %old_block.5, ...), custom_call_target="tpu_custom_call" | custom-call | tf_op jit(solution)/shard_map/pallas_call | solution.py:107
  15.0 0.0 collective-permute-done.1.ov
  15.1 5.6 %collective-permute-start.7 = (bf16[32,64,128]{2,1,0:T(8,128)(2,1)}, bf16[32,64,128]{2,1,0:T(8,128)(2,1)}, u32[]{:S(2)}, u32[]{:S(2)}) collective-permute-start(bf16[32,64,128]{2,1,0:T(8,128)(2,1)} %get-tuple-element.54), channel_id=1, source_target_pairs={{0,64},{16,80},{32,96},{48,112},{64,0},{80,16},{96,32},{112,48},{1... | collective-permute-start | bytes 1572872 | tf_op jit(solution)/shard_map/ppermute | solution.py:139
  20.6 5.5 %attend.1 = bf16[8,576,128]{2,1,0:T(8,128)(2,1)} custom-call(s32[128]{0:T(128)} %old_block.5, s32[64]{0:T(128)} %lengths.1, s32[16]{0:T(128)} %compare_select_fusion.4.base.meta, bf16[64,16,512]{2,1,0:T(8,128)(2,1)} %q, bf16[128,64,128]{2,1,0:T(8,128)(2,1)} %bitcast.14, bf16[128,64,128]{2,1,0:T(8,128)(2,1)} %bitcast.18, bf16[128,64,128]{2,1,0:T(8,128)(2,1)} %copy-done.1, ...), custom_call_target="tpu_custom_call" | custom-call | tf_op jit(solution)/shard_map/attend/pallas_call | solution.py:333
  26.2 0.0 copy-start.7
  26.2 9.1 %all-to-all-start = ((bf16[8,576,128]{2,1,0:T(8,128)(2,1)}), bf16[8,576,128]{2,1,0:T(8,128)(2,1)S(1)}, u32[]{:S(2)}, u32[]{:S(2)}) async-start(bf16[8,576,128]{2,1,0:T(8,128)(2,1)} %attend.1), calls=%async_computation | async-start | bytes 2359296 | tf_op jit(solution)/shard_map/all_to_all | solution.py:399
  35.3 20.6 %collective-permute-done.9 = bf16[32,64,128]{2,1,0:T(8,128)(2,1)} collective-permute-done((bf16[32,64,128]{2,1,0:T(8,128)(2,1)}, bf16[32,64,128]{2,1,0:T(8,128)(2,1)}, u32[]{:S(2)}, u32[]{:S(2)}) %collective-permute-start.9) | collective-permute-done | bytes 524320 | tf_op jit(solution)/shard_map/ppermute | solution.py:139
  55.9 1.2 %slice_add_fusion.6 = (bf16[16,64,128]{2,1,0:T(8,128)(2,1)S(1)}, bf16[16,64,128]{2,1,0:T(8,128)(2,1)S(1)}) fusion(bf16[32,64,128]{2,1,0:T(8,128)(2,1)} %collective-permute-done.9, bf16[32,64,128]{2,1,0:T(8,128)(2,1)} %get-tuple-element.57), kind=kLoop, calls=%fused_computation.13 | loop fusion | flops 262144 | bytes 1572864 | tf_op jit(solution)/shard_map/add | solution.py:156
  57.1 1.1 collective-permute-start.10
  58.2 0.0 collective-permute-done.2
  58.3 2.2 %collective-permute-start.12 = (bf16[16,64,128]{2,1,0:T(8,128)(2,1)S(1)}, bf16[16,64,128]{2,1,0:T(8,128)(2,1)S(1)}, u32[]{:S(2)}, u32[]{:S(2)}) collective-permute-start(bf16[16,64,128]{2,1,0:T(8,128)(2,1)S(1)} %get-tuple-element.67), channel_id=1, source_target_pairs={{16,0},{32,16},{48,32},{0,48},{80,64},{96,80},{112,96},{64,112},{1... | collective-permute-start | bytes 786440 | tf_op jit(solution)/shard_map/ppermute | solution.py:135
  60.5 0.1 slice_add_fusion.2
  60.5 0.0 copy-start.4
  60.5 0.0 collective-permute-done.8
  60.5 0.4 collective-permute-start.5
  60.9 3.9 %collective-permute-done.10 = bf16[16,64,128]{2,1,0:T(8,128)(2,1)S(1)} collective-permute-done((bf16[16,64,128]{2,1,0:T(8,128)(2,1)S(1)}, bf16[16,64,128]{2,1,0:T(8,128)(2,1)S(1)}, u32[]{:S(2)}, u32[]{:S(2)}) %collective-permute-start.10) | collective-permute-done | bytes 262176 | tf_op jit(solution)/shard_map/ppermute | solution.py:129
  64.8 2.6 %collective-permute-done.12 = bf16[16,64,128]{2,1,0:T(8,128)(2,1)S(1)} collective-permute-done((bf16[16,64,128]{2,1,0:T(8,128)(2,1)S(1)}, bf16[16,64,128]{2,1,0:T(8,128)(2,1)S(1)}, u32[]{:S(2)}, u32[]{:S(2)}) %collective-permute-start.12) | collective-permute-done | bytes 262176 | tf_op jit(solution)/shard_map/ppermute | solution.py:135
  67.4 2.3 %fusion.1 = (bf16[32,64,128]{2,1,0:T(8,128)(2,1)}, bf16[32,64,128]{2,1,0:T(8,128)(2,1)}) fusion(bf16[32,64,128]{2,1,0:T(8,128)(2,1)S(1)} %copy-done.5, bf16[64,64,128]{2,1,0:T(8,128)(2,1)} %collective-permute-done.8, bf16[16,64,128]{2,1,0:T(8,128)(2,1)S(1)} %collective-permute-done.10, bf16[16,64,128]{2,1,0:T(8,128)(2,1)S(1)} %collective-permute-done.12, ...), kind=kLoop, calls=%fused_computation.3 | loop fusion | flops 1048576 | bytes 3670016 | tf_op jit(solution)/shard_map/add | solution.py:159
  69.8 1.8 %collective-permute-start.11 = (bf16[32,64,128]{2,1,0:T(8,128)(2,1)}, bf16[32,64,128]{2,1,0:T(8,128)(2,1)}, u32[]{:S(2)}, u32[]{:S(2)}) collective-permute-start(bf16[32,64,128]{2,1,0:T(8,128)(2,1)} %get-tuple-element.64), channel_id=1, source_target_pairs={{0,16},{16,32},{32,48},{48,0},{64,80},{80,96},{96,112},{112,64},{1... | collective-permute-start | bytes 1572872 | tf_op jit(solution)/shard_map/ppermute | solution.py:129
  71.6 1.6 %collective-permute-start.13 = (bf16[32,64,128]{2,1,0:T(8,128)(2,1)}, bf16[32,64,128]{2,1,0:T(8,128)(2,1)}, u32[]{:S(2)}, u32[]{:S(2)}) collective-permute-start(bf16[32,64,128]{2,1,0:T(8,128)(2,1)} %get-tuple-element.65), channel_id=1, source_target_pairs={{16,0},{32,16},{48,32},{0,48},{80,64},{96,80},{112,96},{64,112},{1... | collective-permute-start | bytes 1572872 | tf_op jit(solution)/shard_map/ppermute | solution.py:135
  73.2 0.0 collective-permute-done.3
  73.2 1.9 %slice_add_fusion.3 = bf16[32,64,128]{2,1,0:T(8,128)(2,1)} fusion(bf16[32,64,128]{2,1,0:T(8,128)(2,1)S(1)} %copy-done.4, bf16[64,64,128]{2,1,0:T(8,128)(2,1)} %collective-permute-done.3), kind=kLoop, calls=%fused_computation.5 | loop fusion | flops 262144 | bytes 1572864 | tf_op jit(solution)/shard_map/add | solution.py:145
  75.1 0.4 collective-permute-start.4
  75.5 3.2 %collective-permute-done.5 = bf16[32,64,128]{2,1,0:T(8,128)(2,1)} collective-permute-done((bf16[32,64,128]{2,1,0:T(8,128)(2,1)S(1)}, bf16[32,64,128]{2,1,0:T(8,128)(2,1)}, u32[]{:S(2)}, u32[]{:S(2)}) %collective-permute-start.5) | collective-permute-done | bytes 524320 | tf_op jit(solution)/shard_map/ppermute | solution.py:135
  78.8 0.0 all-to-all-done.got
  78.8 1.0 copy-done
  79.8 3.1 %join.1 = bf16[8,8,16,512]{3,2,1,0:T(8,128)(2,1)} custom-call(bf16[8,576,128]{2,1,0:T(8,128)(2,1)} %copy-done), custom_call_target="tpu_custom_call" | custom-call | tf_op jit(solution)/shard_map/join/pallas_call | solution.py:389
  82.9 7.4 %all-to-all-start.1 = ((bf16[8,8,16,512]{3,2,1,0:T(8,128)(2,1)}), bf16[8,8,16,512]{3,2,1,0:T(8,128)(2,1)S(1)}, u32[]{:S(2)}, u32[]{:S(2)}) async-start(bf16[8,8,16,512]{3,2,1,0:T(8,128)(2,1)} %join.1), calls=%async_computation.1 | async-start | bytes 2097152 | tf_op jit(solution)/shard_map/all_to_all | solution.py:399
  90.3 1.5 %add_add_fusion = bf16[32,64,128]{2,1,0:T(8,128)(2,1)S(1)} fusion(bf16[32,64,128]{2,1,0:T(8,128)(2,1)} %collective-permute-done.5, bf16[32,64,128]{2,1,0:T(8,128)(2,1)} %get-tuple-element.49, bf16[64,64,128]{2,1,0:T(8,128)(2,1)} %collective-permute-done.3), kind=kLoop, calls=%fused_computation.11 | loop fusion | flops 524288 | bytes 2097152 | tf_op jit(solution)/shard_map/add | solution.py:148
  91.8 3.6 %collective-permute-start.6 = (bf16[32,64,128]{2,1,0:T(8,128)(2,1)S(1)}, bf16[32,64,128]{2,1,0:T(8,128)(2,1)S(1)}, u32[]{:S(2)}, u32[]{:S(2)}) collective-permute-start(bf16[32,64,128]{2,1,0:T(8,128)(2,1)S(1)} %add_add_fusion), channel_id=1, source_target_pairs={{0,64},{16,80},{32,96},{48,112},{64,0},{80,16},{96,32},{112,48},{1... | collective-permute-start | bytes 1572872 | tf_op jit(solution)/shard_map/ppermute | solution.py:139
  95.4 0.0 collective-permute-done.7
  95.4 0.0 collective-permute-done.11
  95.4 0.0 collective-permute-done.13
  95.5 2.3 %add_bitcast_fusion = bf16[32,1,64,128]{3,2,1,0:T(8,128)(2,1)} fusion(bf16[32,64,128]{2,1,0:T(8,128)(2,1)} %collective-permute-done.13, bf16[32,64,128]{2,1,0:T(8,128)(2,1)} %collective-permute-done.11, bf16[32,64,128]{2,1,0:T(8,128)(2,1)S(1)} %copy-done.3, bf16[32,64,128]{2,1,0:T(8,128)(2,1)} %collective-permute-done.7), kind=kLoop, calls=%fused_computation.10 | loop fusion | flops 786432 | bytes 2621440
  97.7 0.0 collective-permute-done.4
  97.7 12.3 %collective-permute-done.6 = bf16[32,64,128]{2,1,0:T(8,128)(2,1)S(1)} collective-permute-done((bf16[32,64,128]{2,1,0:T(8,128)(2,1)S(1)}, bf16[32,64,128]{2,1,0:T(8,128)(2,1)S(1)}, u32[]{:S(2)}, u32[]{:S(2)}) %collective-permute-start.6) | collective-permute-done | bytes 524320 | tf_op jit(solution)/shard_map/ppermute | solution.py:139
  110.1 1.9 %fusion.4 = bf16[32,1,64,128]{3,2,1,0:T(8,128)(2,1)} fusion(bf16[32,64,128]{2,1,0:T(8,128)(2,1)S(1)} %collective-permute-done.6, bf16[32,64,128]{2,1,0:T(8,128)(2,1)} %collective-permute-done.4, bf16[32,64,128]{2,1,0:T(8,128)(2,1)S(1)} %copy-done.2, bf16[64,64,128]{2,1,0:T(8,128)(2,1)S(1)} %collective-permute-done.2), kind=kLoop, calls=%fused_computation.9 | loop fusion | flops 786432 | bytes 2621440
  112.0 0.0 all-to-all-done.1
  112.0 1.0 copy.14
  (13 shorter events, 0.0 us)
Async XLA Ops:
  0.6 10.2 %collective-permute-start = (bf16[128,64,128]{2,1,0:T(8,128)(2,1)}, bf16[128,64,128]{2,1,0:T(8,128)(2,1)S(1)}, u32[]{:S(2)}, u32[]{:S(2)}) collective-permute-start(bf16[128,64,128]{2,1,0:T(8,128)(2,1)} %bitcast.11), channel_id=1, source_target_pairs={{0,1},{1,0},{2,3},{3,2},{4,5},{5,4},{6,7},{7,6},{8,9},{9,8},{10,11... | collective-permute-start | bytes 6291464 | tf_op jit(solution)/shard_map/ppermute | solution.py:413
  0.7 14.3 %collective-permute-start.1 = (bf16[128,64,128]{2,1,0:T(8,128)(2,1)}, bf16[128,64,128]{2,1,0:T(8,128)(2,1)}, u32[]{:S(2)}, u32[]{:S(2)}) collective-permute-start(bf16[128,64,128]{2,1,0:T(8,128)(2,1)} %bitcast.15), channel_id=1, source_target_pairs={{0,1},{1,0},{2,3},{3,2},{4,5},{5,4},{6,7},{7,6},{8,9},{9,8},{10,11... | collective-permute-start | bytes 6291464 | tf_op jit(solution)/shard_map/ppermute | solution.py:414
  4.4 53.9 %collective-permute-start.2 = (bf16[64,64,128]{2,1,0:T(8,128)(2,1)}, bf16[64,64,128]{2,1,0:T(8,128)(2,1)S(1)}, u32[]{:S(2)}, u32[]{:S(2)}) collective-permute-start(bf16[64,64,128]{2,1,0:T(8,128)(2,1)} %get-tuple-element.46), channel_id=1, source_target_pairs={{16,0},{32,16},{48,32},{0,48},{80,64},{96,80},{112,96},{64,112},{1... | collective-permute-start | bytes 3145736 | tf_op jit(solution)/shard_map/ppermute | solution.py:135
  7.3 53.2 %collective-permute-start.8 = (bf16[64,64,128]{2,1,0:T(8,128)(2,1)}, bf16[64,64,128]{2,1,0:T(8,128)(2,1)}, u32[]{:S(2)}, u32[]{:S(2)}) collective-permute-start(bf16[64,64,128]{2,1,0:T(8,128)(2,1)} %get-tuple-element.56), channel_id=1, source_target_pairs={{0,64},{16,80},{32,96},{48,112},{64,0},{80,16},{96,32},{112,48},{1... | collective-permute-start | bytes 3145736 | tf_op jit(solution)/shard_map/ppermute | solution.py:139
  10.5 45.4 %collective-permute-start.9 = (bf16[32,64,128]{2,1,0:T(8,128)(2,1)}, bf16[32,64,128]{2,1,0:T(8,128)(2,1)}, u32[]{:S(2)}, u32[]{:S(2)}) collective-permute-start(bf16[32,64,128]{2,1,0:T(8,128)(2,1)} %get-tuple-element.58), channel_id=1, source_target_pairs={{0,64},{16,80},{32,96},{48,112},{64,0},{80,16},{96,32},{112,48},{1... | collective-permute-start | bytes 1572872 | tf_op jit(solution)/shard_map/ppermute | solution.py:139
  10.9 4.2 %copy-start.1 = (bf16[128,64,128]{2,1,0:T(8,128)(2,1)}, bf16[128,64,128]{2,1,0:T(8,128)(2,1)S(1)}, u32[]{:S(2)}) copy-start(bf16[128,64,128]{2,1,0:T(8,128)(2,1)S(1)} %collective-permute-done.ok) | copy-start | bytes 6291460
  10.9 62.3 %collective-permute-start.3 = (bf16[64,64,128]{2,1,0:T(8,128)(2,1)}, bf16[64,64,128]{2,1,0:T(8,128)(2,1)}, u32[]{:S(2)}, u32[]{:S(2)}) collective-permute-start(bf16[64,64,128]{2,1,0:T(8,128)(2,1)} %get-tuple-element.48), channel_id=1, source_target_pairs={{0,16},{16,32},{32,48},{48,0},{64,80},{80,96},{96,112},{112,64},{1... | collective-permute-start | bytes 3145736 | tf_op jit(solution)/shard_map/ppermute | solution.py:129
  15.1 80.4 %collective-permute-start.7 = (bf16[32,64,128]{2,1,0:T(8,128)(2,1)}, bf16[32,64,128]{2,1,0:T(8,128)(2,1)}, u32[]{:S(2)}, u32[]{:S(2)}) collective-permute-start(bf16[32,64,128]{2,1,0:T(8,128)(2,1)} %get-tuple-element.54), channel_id=1, source_target_pairs={{0,64},{16,80},{32,96},{48,112},{64,0},{80,16},{96,32},{112,48},{1... | collective-permute-start | bytes 1572872 | tf_op jit(solution)/shard_map/ppermute | solution.py:139
  26.2 34.3 %copy-start.7 = (bf16[32,64,128]{2,1,0:T(8,128)(2,1)S(1)}, bf16[32,64,128]{2,1,0:T(8,128)(2,1)}, u32[]{:S(2)}) copy-start(bf16[32,64,128]{2,1,0:T(8,128)(2,1)} %get-tuple-element.50) | copy-start | bytes 1572868
  26.2 52.6 %all-to-all-start = ((bf16[8,576,128]{2,1,0:T(8,128)(2,1)}), bf16[8,576,128]{2,1,0:T(8,128)(2,1)S(1)}, u32[]{:S(2)}, u32[]{:S(2)}) async-start(bf16[8,576,128]{2,1,0:T(8,128)(2,1)} %attend.1), calls=%async_computation | async-start | bytes 2359296 | tf_op jit(solution)/shard_map/all_to_all | solution.py:399
  35.3 32.2 %copy-start.5 = (bf16[32,64,128]{2,1,0:T(8,128)(2,1)S(1)}, bf16[32,64,128]{2,1,0:T(8,128)(2,1)}, u32[]{:S(2)}) copy-start(bf16[32,64,128]{2,1,0:T(8,128)(2,1)} %get-tuple-element.55) | copy-start | bytes 1572868
  35.3 32.2 %copy-start.6 = (bf16[32,64,128]{2,1,0:T(8,128)(2,1)S(1)}, bf16[32,64,128]{2,1,0:T(8,128)(2,1)}, u32[]{:S(2)}) copy-start(bf16[32,64,128]{2,1,0:T(8,128)(2,1)} %get-tuple-element.59) | copy-start | bytes 1572868
  57.1 7.7 %collective-permute-start.10 = (bf16[16,64,128]{2,1,0:T(8,128)(2,1)S(1)}, bf16[16,64,128]{2,1,0:T(8,128)(2,1)S(1)}, u32[]{:S(2)}, u32[]{:S(2)}) collective-permute-start(bf16[16,64,128]{2,1,0:T(8,128)(2,1)S(1)} %get-tuple-element.66), channel_id=1, source_target_pairs={{0,16},{16,32},{32,48},{48,0},{64,80},{80,96},{96,112},{112,64},{1... | collective-permute-start | bytes 786440 | tf_op jit(solution)/shard_map/ppermute | solution.py:129
  58.3 9.2 %collective-permute-start.12 = (bf16[16,64,128]{2,1,0:T(8,128)(2,1)S(1)}, bf16[16,64,128]{2,1,0:T(8,128)(2,1)S(1)}, u32[]{:S(2)}, u32[]{:S(2)}) collective-permute-start(bf16[16,64,128]{2,1,0:T(8,128)(2,1)S(1)} %get-tuple-element.67), channel_id=1, source_target_pairs={{16,0},{32,16},{48,32},{0,48},{80,64},{96,80},{112,96},{64,112},{1... | collective-permute-start | bytes 786440 | tf_op jit(solution)/shard_map/ppermute | solution.py:135
  60.5 12.7 %copy-start.4 = (bf16[32,64,128]{2,1,0:T(8,128)(2,1)S(1)}, bf16[32,64,128]{2,1,0:T(8,128)(2,1)}, u32[]{:S(2)}) copy-start(bf16[32,64,128]{2,1,0:T(8,128)(2,1)} %get-tuple-element.47) | copy-start | bytes 1572868
  60.5 18.2 %collective-permute-start.5 = (bf16[32,64,128]{2,1,0:T(8,128)(2,1)S(1)}, bf16[32,64,128]{2,1,0:T(8,128)(2,1)}, u32[]{:S(2)}, u32[]{:S(2)}) collective-permute-start(bf16[32,64,128]{2,1,0:T(8,128)(2,1)S(1)} %slice_add_fusion.2), channel_id=1, source_target_pairs={{16,0},{32,16},{48,32},{0,48},{80,64},{96,80},{112,96},{64,112},{1... | collective-permute-start | bytes 1572872 | tf_op jit(solution)/shard_map/ppermute | solution.py:135
  69.8 25.7 %collective-permute-start.11 = (bf16[32,64,128]{2,1,0:T(8,128)(2,1)}, bf16[32,64,128]{2,1,0:T(8,128)(2,1)}, u32[]{:S(2)}, u32[]{:S(2)}) collective-permute-start(bf16[32,64,128]{2,1,0:T(8,128)(2,1)} %get-tuple-element.64), channel_id=1, source_target_pairs={{0,16},{16,32},{32,48},{48,0},{64,80},{80,96},{96,112},{112,64},{1... | collective-permute-start | bytes 1572872 | tf_op jit(solution)/shard_map/ppermute | solution.py:129
  71.6 23.8 %collective-permute-start.13 = (bf16[32,64,128]{2,1,0:T(8,128)(2,1)}, bf16[32,64,128]{2,1,0:T(8,128)(2,1)}, u32[]{:S(2)}, u32[]{:S(2)}) collective-permute-start(bf16[32,64,128]{2,1,0:T(8,128)(2,1)} %get-tuple-element.65), channel_id=1, source_target_pairs={{16,0},{32,16},{48,32},{0,48},{80,64},{96,80},{112,96},{64,112},{1... | collective-permute-start | bytes 1572872 | tf_op jit(solution)/shard_map/ppermute | solution.py:135
  75.1 22.6 %collective-permute-start.4 = (bf16[32,64,128]{2,1,0:T(8,128)(2,1)}, bf16[32,64,128]{2,1,0:T(8,128)(2,1)}, u32[]{:S(2)}, u32[]{:S(2)}) collective-permute-start(bf16[32,64,128]{2,1,0:T(8,128)(2,1)} %slice_add_fusion.3), channel_id=1, source_target_pairs={{0,16},{16,32},{32,48},{48,0},{64,80},{80,96},{96,112},{112,64},{1... | collective-permute-start | bytes 1572872 | tf_op jit(solution)/shard_map/ppermute | solution.py:129
  78.8 1.0 copy-start
  82.9 12.6 %copy-start.3 = (bf16[32,64,128]{2,1,0:T(8,128)(2,1)S(1)}, bf16[32,64,128]{2,1,0:T(8,128)(2,1)}, u32[]{:S(2)}) copy-start(bf16[32,64,128]{2,1,0:T(8,128)(2,1)} %get-tuple-element.53) | copy-start | bytes 1572868
  82.9 29.1 %all-to-all-start.1 = ((bf16[8,8,16,512]{3,2,1,0:T(8,128)(2,1)}), bf16[8,8,16,512]{3,2,1,0:T(8,128)(2,1)S(1)}, u32[]{:S(2)}, u32[]{:S(2)}) async-start(bf16[8,8,16,512]{3,2,1,0:T(8,128)(2,1)} %join.1), calls=%async_computation.1 | async-start | bytes 2097152 | tf_op jit(solution)/shard_map/all_to_all | solution.py:399
  90.3 19.7 %copy-start.2 = (bf16[32,64,128]{2,1,0:T(8,128)(2,1)S(1)}, bf16[32,64,128]{2,1,0:T(8,128)(2,1)}, u32[]{:S(2)}) copy-start(bf16[32,64,128]{2,1,0:T(8,128)(2,1)} %get-tuple-element.45) | copy-start | bytes 1572868
  91.8 18.2 %collective-permute-start.6 = (bf16[32,64,128]{2,1,0:T(8,128)(2,1)S(1)}, bf16[32,64,128]{2,1,0:T(8,128)(2,1)S(1)}, u32[]{:S(2)}, u32[]{:S(2)}) collective-permute-start(bf16[32,64,128]{2,1,0:T(8,128)(2,1)S(1)} %add_add_fusion), channel_id=1, source_target_pairs={{0,64},{16,80},{32,96},{48,112},{64,0},{80,16},{96,32},{112,48},{1... | collective-permute-start | bytes 1572872 | tf_op jit(solution)/shard_map/ppermute | solution.py:139
where the time goes:
time: 114 us; the launch traced here: 113 us
  waiting for transfers between devices  42.7 us (37%)
  starting transfers between devices  41.4 us (36%)
  Pallas kernels  14.3 us (13%)
  other arithmetic  11.7 us (10%)
  local copies, waits for them, and re-layouts  2.03 us (2%)
    ppermute x4, waiting for transfers between devices, across(): lax.ppermute(x, 'inst', [(i, i ^ COLS) for i in range(lax.axis_size('inst...  33 us
    all_to_all x2, starting transfers between devices, spread(): return lax.all_to_all(x, 'inst', split_axis=0, concat_axis=0, tiled=True)  16.5 us
    ppermute x4, starting transfers between devices, across(): lax.ppermute(x, 'inst', [(i, i ^ COLS) for i in range(lax.axis_size('inst...  12.7 us
    ppermute x4, starting transfers between devices, left(): return lax.ppermute(x, 'inst', route)  7.11 us
    ppermute x4, waiting for transfers between devices, left(): return lax.ppermute(x, 'inst', route)  5.89 us
    pallas_call x2, Pallas kernels, pack(): pl.pallas_call(functools.partial(pack_body, groups_k, groups_v), in_specs...  5.69 us
    pallas_call x1, Pallas kernels, attend(): pl.pallas_call(attend_body, in_specs=[smem] * 3 + [anyspace] * 7, out_spe...  5.51 us
    ppermute x4, starting transfers between devices, right(): return lax.ppermute(x, 'inst', route)  4.48 us
  transfers between devices with their start and end apart: 16, of which 5 were waited for; matrix products, arithmetic and copies ran while one was open for 10% of the time, Pallas kernels for 13%

commit v1 on v0

--- a/solution.py
+++ b/solution.py
@@ -316,7 +316,7 @@
     lax.fori_loop(0, insts, finish, 0)
 
 
-UNROLL = 16
+UNROLL = 32
 SETTLE = 16
 
 
@@ -357,9 +357,8 @@
 
 def join_body(got, out):
     insts, _, head_dim = got.shape
-    rows = out.shape[1]
-    draft = out.shape[2]
-    heads = out.shape[3] // head_dim
+    rows, draft, width = out.shape
+    heads = width // head_dim
     qrows = draft * heads
     lane = lax.broadcasted_iota(jnp.int32, (qrows, head_dim), 1)
     stats = [got[s, rows * qrows :, :].astype(jnp.float32) for s in range(insts)]
@@ -378,21 +377,56 @@
             total = total + share
             acc = acc + share * got[s, a * qrows : (a + 1) * qrows, :].astype(jnp.float32)
         res = (acc / total).astype(out.dtype)
-        for d in range(insts):
-            for h in range(heads):
-                out[d, a, :, h * head_dim : (h + 1) * head_dim] = res[h * draft : (h + 1) * draft]
+        for h in range(heads):
+            out[a, :, h * head_dim : (h + 1) * head_dim] = res[h * draft : (h + 1) * draft]
 
 
 def join(got, rows, draft, width):
-    insts = got.shape[0]
     vmem = pl.BlockSpec(memory_space=pltpu.VMEM)
     return pl.pallas_call(
         join_body,
         in_specs=[vmem],
         out_specs=vmem,
-        out_shape=jax.ShapeDtypeStruct((insts, rows, draft, width), got.dtype),
+        out_shape=jax.ShapeDtypeStruct((rows, draft, width), got.dtype),
         name="join",
     )(got)
+
+
+def place_body(per, table, pair, east, far_own, far_other, west, out, sems):
+    rows = far_own.shape[0]
+    pieces = (
+        pair.at[:rows], pair.at[rows:], east.at[:rows], east.at[rows:],
+        far_own, far_other, west.at[:rows], west.at[rows:],
+    )
+    copies = [
+        pltpu.make_async_copy(
+            piece, out.at[pl.ds(table[p] // per * rows, rows)], sems.at[p]
+        )
+        for p, piece in enumerate(pieces)
+    ]
+    for copy in copies:
+        copy.start()
+    for copy in copies:
+        copy.wait()
+
+
+def results(mine, table, per, shape):
+    rows = mine.shape[0]
+    other = across(mine)
+    pair = jnp.concatenate([mine, other])
+    west = right(pair)
+    east = left(pair)
+    far_own = right(west[:rows])
+    far_other = left(east[rows:])
+    vmem = pl.BlockSpec(memory_space=pltpu.VMEM)
+    return pl.pallas_call(
+        functools.partial(place_body, per),
+        in_specs=[pl.BlockSpec(memory_space=pltpu.SMEM)] + [vmem] * 5,
+        out_specs=pl.BlockSpec(memory_space=pl.ANY),
+        out_shape=jax.ShapeDtypeStruct(shape, mine.dtype),
+        scratch_shapes=[pltpu.SemaphoreType.DMA((8,))],
+        name="place",
+    )(table, pair, east, far_own, far_other, west)
 
 
 def spread(x):
@@ -414,14 +448,16 @@
     other_v = lax.ppermute(values, "head", swap)
 
     table = table_of(blocks // insts, rows, half, head_dim)
-    out_k, out_v = pack(old_block, new_slot, table, keys, values, insts, SENT_K, SENT_V)
+    out_k, out_v = pack(
+        old_block, new_slot, table, keys, values, insts, SENT_K + KEPT_K, SENT_V + KEPT_V
+    )
     queries, out_k, out_v = lax.optimization_barrier((queries, out_k, out_v))
     shape = (blocks // insts, entries, half, head_dim)
     far2 = across(out_v[0])
     from_left = right(out_k[0])
     from_right = left(out_k[1])
     far = across(out_v[1])
-    kept_k, kept_v = pack(old_block, new_slot, table, keys, values, insts, KEPT_K, KEPT_V)
+    kept_k, kept_v = out_k[len(SENT_K) :], out_v[len(SENT_V) :]
     near = across(kept_v[0])
     packet = attend(
         old_block, lengths, table, queries, keys, values, other_k, other_v,
@@ -432,7 +468,7 @@
     moved_values = move_values(far2, far, near, rest_v).reshape(shape)
     got = spread(packet)
     mine = join(got, rows, queries.shape[1], queries.shape[2])
-    attended = spread(mine).reshape(queries.shape)
+    attended = results(mine, table, blocks // insts, queries.shape)
     return moved_keys, moved_values, attended
 
 

time: 114 us -> 114 us (level)
    all_to_all x2 -> x1, starting transfers between devices: 16.5 us -> 8.24 us  [spread(): return lax.all_to_all(x, 'inst', split_axis=0, concat_axis=0, tiled=True)]
    ppermute x4 -> x6, starting transfers between devices: 7.11 us -> 13.6 us  [left(): return lax.ppermute(x, 'inst', route)]
    ppermute x4 -> x6, waiting for transfers between devices: 3.88 us -> 6.93 us  [right(): return lax.ppermute(x, 'inst', route)]
    ppermute x4 -> x5, waiting for transfers between devices: 33 us -> 29.9 us  [across(): lax.ppermute(x, 'inst', [(i, i ^ COLS) for i in range(lax.axis_size('inst...]
    pallas_call x0 -> x1, Pallas kernels: none -> 2.25 us  [results(): pl.pallas_call(functools.partial(place_body, per), in_specs=[pl.BlockSpec...]
    pallas_call x2 -> x1, Pallas kernels: 5.69 us -> 4.18 us  [pack(): pl.pallas_call(functools.partial(pack_body, groups_k, groups_v), in_specs...]
    ppermute x4 -> x5, starting transfers between devices: 12.7 us -> 14 us  [across(): lax.ppermute(x, 'inst', [(i, i ^ COLS) for i in range(lax.axis_size('inst...]
    unnamed x17 -> x28, local copies, waits for them, and re-layouts: 2.03 us -> 2.36 us
  transfers between devices with their start and end apart: 16 -> 20, of which waited for: 5 -> 7; matrix products, arithmetic and copies ran while one was open for 10% -> 10% of each run, Pallas kernels for 13% -> 11%
where the time goes in v1:
time: 114 us; the launch traced here: 113 us
  waiting for transfers between devices  42.7 us (37%)
  starting transfers between devices  40.9 us (36%)
  Pallas kernels  14.7 us (13%)
  other arithmetic  11.7 us (10%)
  local copies, waits for them, and re-layouts  2.38 us (2%)
    ppermute x5, waiting for transfers between devices, across(): lax.ppermute(x, 'inst', [(i, i ^ COLS) for i in range(lax.axis_size('inst...  29.9 us
    ppermute x5, starting transfers between devices, across(): lax.ppermute(x, 'inst', [(i, i ^ COLS) for i in range(lax.axis_size('inst...  14 us
    ppermute x6, starting transfers between devices, left(): return lax.ppermute(x, 'inst', route)  13.6 us
    all_to_all x1, starting transfers between devices, spread(): return lax.all_to_all(x, 'inst', split_axis=0, concat_axis=0, tiled=True)  8.24 us
    ppermute x6, waiting for transfers between devices, right(): return lax.ppermute(x, 'inst', route)  6.93 us
    ppermute x6, waiting for transfers between devices, left(): return lax.ppermute(x, 'inst', route)  5.79 us
    pallas_call x1, Pallas kernels, attend(): pl.pallas_call(attend_body, in_specs=[smem] * 3 + [anyspace] * 7, out_spe...  5.51 us
    ppermute x6, starting transfers between devices, right(): return lax.ppermute(x, 'inst', route)  4.45 us
  transfers between devices with their start and end apart: 20, of which 7 were waited for; matrix products, arithmetic and copies ran while one was open for 10% of the time, Pallas kernels for 11%

profile of v1, /device:TPU:0, one launch (start us, length us, event | category | flops | bytes accessed | tf_op | source)
XLA Modules:
  0.0 113.1 jit_solution(9838360657313139554)
XLA Ops:
  0.6 0.1 collective-permute-start
  0.7 0.5 collective-permute-start.1
  1.2 0.5 compare_select_fusion.4.base.meta.table
  1.7 4.2 %shard_map.103 = (bf16[64,64,128]{2,1,0:T(8,128)(2,1)}, bf16[64,64,128]{2,1,0:T(8,128)(2,1)}, bf16[32,64,128]{2,1,0:T(8,128)(2,1)}, bf16[32,64,128]{2,1,0:T(8,12...) custom-call(s32[128]{0:T(128)} %old_block.3, ...), custom_call_target="tpu_custom_call" | custom-call | tf_op jit(solution)/shard_map/pallas_call | solution.py:107
  5.9 2.9 %collective-permute-start.2 = (bf16[64,64,128]{2,1,0:T(8,128)(2,1)}, bf16[64,64,128]{2,1,0:T(8,128)(2,1)S(1)}, u32[]{:S(2)}, u32[]{:S(2)}) collective-permute-start(bf16[64,64,128]{2,1,0:T(8,128)(2,1)} %get-tuple-element.64), channel_id=1, source_target_pairs={{16,0},{32,16},{48,32},{0,48},{80,64},{96,80},{112,96},{64,112},{1... | collective-permute-start | bytes 3145736 | tf_op jit(solution)/shard_map/ppermute | solution.py:135
  8.9 3.2 %collective-permute-start.8 = (bf16[64,64,128]{2,1,0:T(8,128)(2,1)}, bf16[64,64,128]{2,1,0:T(8,128)(2,1)}, u32[]{:S(2)}, u32[]{:S(2)}) collective-permute-start(bf16[64,64,128]{2,1,0:T(8,128)(2,1)} %get-tuple-element.74), channel_id=1, source_target_pairs={{0,64},{16,80},{32,96},{48,112},{64,0},{80,16},{96,32},{112,48},{1... | collective-permute-start | bytes 3145736 | tf_op jit(solution)/shard_map/ppermute | solution.py:139
  12.1 0.3 collective-permute-start.9
  12.4 1.0 collective-permute-start.3
  13.4 3.5 %collective-permute-start.7 = (bf16[32,64,128]{2,1,0:T(8,128)(2,1)}, bf16[32,64,128]{2,1,0:T(8,128)(2,1)}, u32[]{:S(2)}, u32[]{:S(2)}) collective-permute-start(bf16[32,64,128]{2,1,0:T(8,128)(2,1)} %get-tuple-element.72), channel_id=1, source_target_pairs={{0,64},{16,80},{32,96},{48,112},{64,0},{80,16},{96,32},{112,48},{1... | collective-permute-start | bytes 1572872 | tf_op jit(solution)/shard_map/ppermute | solution.py:139
  16.9 5.5 %attend.1 = bf16[8,576,128]{2,1,0:T(8,128)(2,1)} custom-call(s32[128]{0:T(128)} %old_block.3, s32[64]{0:T(128)} %lengths.1, s32[16]{0:T(128)} %compare_select_fusion.4.base.meta.table, bf16[64,16,512]{2,1,0:T(8,128)(2,1)} %q, bf16[128,64,128]{2,1,0:T(8,128)(2,1)} %bitcast.12, bf16[128,64,128]{2,1,0:T(8,128)(2,1)} %bitcast.15, ...), custom_call_target="tpu_custom_call" | custom-call | tf_op jit(solution)/shard_map/attend/pallas_call | solution.py:333
  22.4 0.0 copy-start.10
  22.4 8.2 %all-to-all-start = ((bf16[8,576,128]{2,1,0:T(8,128)(2,1)}), bf16[8,576,128]{2,1,0:T(8,128)(2,1)S(1)}, u32[]{:S(2)}, u32[]{:S(2)}) async-start(bf16[8,576,128]{2,1,0:T(8,128)(2,1)} %attend.1), calls=%async_computation | async-start | bytes 2359296 | tf_op jit(solution)/shard_map/all_to_all | solution.py:433
  30.7 26.8 %collective-permute-done.9 = bf16[32,64,128]{2,1,0:T(8,128)(2,1)} collective-permute-done((bf16[32,64,128]{2,1,0:T(8,128)(2,1)}, bf16[32,64,128]{2,1,0:T(8,128)(2,1)}, u32[]{:S(2)}, u32[]{:S(2)}) %collective-permute-start.9) | collective-permute-done | bytes 524320 | tf_op jit(solution)/shard_map/ppermute | solution.py:139
  57.4 1.2 %slice_add_fusion.6 = (bf16[16,64,128]{2,1,0:T(8,128)(2,1)S(1)}, bf16[16,64,128]{2,1,0:T(8,128)(2,1)S(1)}) fusion(bf16[32,64,128]{2,1,0:T(8,128)(2,1)} %collective-permute-done.9, bf16[32,64,128]{2,1,0:T(8,128)(2,1)} %get-tuple-element.75), kind=kLoop, calls=%fused_computation.13 | loop fusion | flops 262144 | bytes 1572864 | tf_op jit(solution)/shard_map/add | solution.py:156
  58.7 1.0 collective-permute-start.10
  59.7 0.0 collective-permute-done.2
  59.7 2.3 %collective-permute-start.12 = (bf16[16,64,128]{2,1,0:T(8,128)(2,1)S(1)}, bf16[16,64,128]{2,1,0:T(8,128)(2,1)S(1)}, u32[]{:S(2)}, u32[]{:S(2)}) collective-permute-start(bf16[16,64,128]{2,1,0:T(8,128)(2,1)S(1)} %get-tuple-element.85), channel_id=1, source_target_pairs={{16,0},{32,16},{48,32},{0,48},{80,64},{96,80},{112,96},{64,112},{1... | collective-permute-start | bytes 786440 | tf_op jit(solution)/shard_map/ppermute | solution.py:135
  62.0 0.1 slice_add_fusion.2
  62.0 0.0 copy-start.7
  62.1 0.3 collective-permute-start.5
  62.4 4.0 %collective-permute-done.10 = bf16[16,64,128]{2,1,0:T(8,128)(2,1)S(1)} collective-permute-done((bf16[16,64,128]{2,1,0:T(8,128)(2,1)S(1)}, bf16[16,64,128]{2,1,0:T(8,128)(2,1)S(1)}, u32[]{:S(2)}, u32[]{:S(2)}) %collective-permute-start.10) | collective-permute-done | bytes 262176 | tf_op jit(solution)/shard_map/ppermute | solution.py:129
  66.3 2.5 %collective-permute-done.12 = bf16[16,64,128]{2,1,0:T(8,128)(2,1)S(1)} collective-permute-done((bf16[16,64,128]{2,1,0:T(8,128)(2,1)S(1)}, bf16[16,64,128]{2,1,0:T(8,128)(2,1)S(1)}, u32[]{:S(2)}, u32[]{:S(2)}) %collective-permute-start.12) | collective-permute-done | bytes 262176 | tf_op jit(solution)/shard_map/ppermute | solution.py:135
  68.9 2.3 %fusion.1 = (bf16[32,64,128]{2,1,0:T(8,128)(2,1)}, bf16[32,64,128]{2,1,0:T(8,128)(2,1)}) fusion(bf16[32,64,128]{2,1,0:T(8,128)(2,1)S(1)} %copy-done.8, bf16[64,64,128]{2,1,0:T(8,128)(2,1)} %collective-permute-done.8, bf16[16,64,128]{2,1,0:T(8,128)(2,1)S(1)} %collective-permute-done.10, bf16[16,64,128]{2,1,0:T(8,128)(2,1)S(1)} %collective-permute-done.12, ...), kind=kLoop, calls=%fused_computation.3 | loop fusion | flops 1048576 | bytes 3670016 | tf_op jit(solution)/shard_map/add | solution.py:159
  71.2 1.8 %collective-permute-start.11 = (bf16[32,64,128]{2,1,0:T(8,128)(2,1)}, bf16[32,64,128]{2,1,0:T(8,128)(2,1)}, u32[]{:S(2)}, u32[]{:S(2)}) collective-permute-start(bf16[32,64,128]{2,1,0:T(8,128)(2,1)} %get-tuple-element.82), channel_id=1, source_target_pairs={{0,16},{16,32},{32,48},{48,0},{64,80},{80,96},{96,112},{112,64},{1... | collective-permute-start | bytes 1572872 | tf_op jit(solution)/shard_map/ppermute | solution.py:129
  73.1 1.7 %collective-permute-start.13 = (bf16[32,64,128]{2,1,0:T(8,128)(2,1)}, bf16[32,64,128]{2,1,0:T(8,128)(2,1)}, u32[]{:S(2)}, u32[]{:S(2)}) collective-permute-start(bf16[32,64,128]{2,1,0:T(8,128)(2,1)} %get-tuple-element.83), channel_id=1, source_target_pairs={{16,0},{32,16},{48,32},{0,48},{80,64},{96,80},{112,96},{64,112},{1... | collective-permute-start | bytes 1572872 | tf_op jit(solution)/shard_map/ppermute | solution.py:135
  74.7 0.0 collective-permute-done.3
  74.7 1.9 %slice_add_fusion.3 = bf16[32,64,128]{2,1,0:T(8,128)(2,1)} fusion(bf16[32,64,128]{2,1,0:T(8,128)(2,1)S(1)} %copy-done.7, bf16[64,64,128]{2,1,0:T(8,128)(2,1)} %collective-permute-done.3), kind=kLoop, calls=%fused_computation.5 | loop fusion | flops 262144 | bytes 1572864 | tf_op jit(solution)/shard_map/add | solution.py:145
  76.6 0.3 collective-permute-start.4
  77.0 3.2 %collective-permute-done.5 = bf16[32,64,128]{2,1,0:T(8,128)(2,1)} collective-permute-done((bf16[32,64,128]{2,1,0:T(8,128)(2,1)S(1)}, bf16[32,64,128]{2,1,0:T(8,128)(2,1)}, u32[]{:S(2)}, u32[]{:S(2)}) %collective-permute-start.5) | collective-permute-done | bytes 524320 | tf_op jit(solution)/shard_map/ppermute | solution.py:135
  80.2 1.0 copy-done
  81.3 2.7 %join.1 = bf16[8,16,512]{2,1,0:T(8,128)(2,1)} custom-call(bf16[8,576,128]{2,1,0:T(8,128)(2,1)} %copy-done), custom_call_target="tpu_custom_call" | custom-call | tf_op jit(solution)/shard_map/join/pallas_call | solution.py:386
  84.0 3.5 %collective-permute-start.14 = (bf16[8,16,512]{2,1,0:T(8,128)(2,1)}, bf16[8,16,512]{2,1,0:T(8,128)(2,1)S(1)}, u32[]{:S(2)}, u32[]{:S(2)}) collective-permute-start(bf16[8,16,512]{2,1,0:T(8,128)(2,1)} %join.1), channel_id=1, source_target_pairs={{0,64},{16,80},{32,96},{48,112},{64,0},{80,16},{96,32},{112,48},{1... | collective-permute-start | bytes 393224 | tf_op jit(solution)/shard_map/ppermute | solution.py:139
  87.5 1.4 %add_add_fusion = bf16[32,64,128]{2,1,0:T(8,128)(2,1)S(1)} fusion(bf16[32,64,128]{2,1,0:T(8,128)(2,1)} %collective-permute-done.5, bf16[32,64,128]{2,1,0:T(8,128)(2,1)} %get-tuple-element.67, bf16[64,64,128]{2,1,0:T(8,128)(2,1)} %collective-permute-done.3), kind=kLoop, calls=%fused_computation.11 | loop fusion | flops 524288 | bytes 2097152 | tf_op jit(solution)/shard_map/add | solution.py:148
  89.0 3.2 %collective-permute-done.14 = bf16[8,16,512]{2,1,0:T(8,128)(2,1)S(1)} collective-permute-done((bf16[8,16,512]{2,1,0:T(8,128)(2,1)}, bf16[8,16,512]{2,1,0:T(8,128)(2,1)S(1)}, u32[]{:S(2)}, u32[]{:S(2)}) %collective-permute-start.14) | collective-permute-done | bytes 131104 | tf_op jit(solution)/shard_map/ppermute | solution.py:139
  92.2 3.5 %collective-permute-start.6 = (bf16[32,64,128]{2,1,0:T(8,128)(2,1)S(1)}, bf16[32,64,128]{2,1,0:T(8,128)(2,1)S(1)}, u32[]{:S(2)}, u32[]{:S(2)}) collective-permute-start(bf16[32,64,128]{2,1,0:T(8,128)(2,1)S(1)} %add_add_fusion), channel_id=1, source_target_pairs={{0,64},{16,80},{32,96},{48,112},{64,0},{80,16},{96,32},{112,48},{1... | collective-permute-start | bytes 1572872 | tf_op jit(solution)/shard_map/ppermute | solution.py:139
  95.7 0.0 collective-permute-done.7
  95.7 0.2 collective-permute-start.16
  95.8 0.0 collective-permute-done.11
  95.8 3.2 %collective-permute-start.15 = (bf16[16,16,512]{2,1,0:T(8,128)(2,1)S(1)}, bf16[16,16,512]{2,1,0:T(8,128)(2,1)S(1)}, u32[]{:S(2)}, u32[]{:S(2)}) collective-permute-start(bf16[16,16,512]{2,1,0:T(8,128)(2,1)S(1)} %pad_maximum_fusion.pair), channel_id=1, source_target_pairs={{16,0},{32,16},{48,32},{0,48},{80,64},{96,80},{112,96},{64,112},{1... | collective-permute-start | bytes 786440 | tf_op jit(solution)/shard_map/ppermute | solution.py:135
  99.0 2.3 %add_bitcast_fusion = bf16[32,1,64,128]{3,2,1,0:T(8,128)(2,1)} fusion(bf16[32,64,128]{2,1,0:T(8,128)(2,1)} %collective-permute-done.13, bf16[32,64,128]{2,1,0:T(8,128)(2,1)} %collective-permute-done.11, bf16[32,64,128]{2,1,0:T(8,128)(2,1)S(1)} %copy-done.6, bf16[32,64,128]{2,1,0:T(8,128)(2,1)} %collective-permute-done.7), kind=kLoop, calls=%fused_computation.10 | loop fusion | flops 786432 | bytes 2621440
  101.3 2.1 %collective-permute-done.16.west = bf16[16,16,512]{2,1,0:T(8,128)(2,1)S(1)} collective-permute-done((bf16[16,16,512]{2,1,0:T(8,128)(2,1)S(1)}, bf16[16,16,512]{2,1,0:T(8,128)(2,1)S(1)}, u32[]{:S(2)}, u32[]{:S(2)}) %collective-permute-start.16) | collective-permute-done | bytes 262176 | tf_op jit(solution)/shard_map/ppermute | solution.py:129
  103.3 0.1 collective-permute-start.17
  103.5 3.3 %collective-permute-start.18 = (bf16[8,16,512]{2,1,0:T(8,128)(2,1)S(1)}, bf16[8,16,512]{2,1,0:T(8,128)(2,1)S(1)}, u32[]{:S(2)}, u32[]{:S(2)}) collective-permute-start(bf16[8,16,512]{2,1,0:T(8,128)(2,1)S(1)} %slice.56), channel_id=1, source_target_pairs={{16,0},{32,16},{48,32},{0,48},{80,64},{96,80},{112,96},{64,112},{1... | collective-permute-start | bytes 393224 | tf_op jit(solution)/shard_map/ppermute | solution.py:135
  106.7 1.9 %fusion.4 = bf16[32,1,64,128]{3,2,1,0:T(8,128)(2,1)} fusion(bf16[32,64,128]{2,1,0:T(8,128)(2,1)S(1)} %collective-permute-done.6, bf16[32,64,128]{2,1,0:T(8,128)(2,1)} %collective-permute-done.4, bf16[32,64,128]{2,1,0:T(8,128)(2,1)S(1)} %copy-done.5, bf16[64,64,128]{2,1,0:T(8,128)(2,1)S(1)} %collective-permute-done.2), kind=kLoop, calls=%fused_computation.9 | loop fusion | flops 786432 | bytes 2621440
  108.7 0.9 collective-permute-done.17.far_own
  109.6 0.6 copy-done.12
  110.2 0.7 copy-done.13
  110.9 2.3 %place.1 = bf16[64,16,512]{2,1,0:T(8,128)(2,1)} custom-call(s32[16]{0:T(128)} %compare_select_fusion.4.base.meta.table, bf16[16,16,512]{2,1,0:T(8,128)(2,1)} %copy-done.2, bf16[16,16,512]{2,1,0:T(8,128)(2,1)} %copy-done.4, bf16[8,16,512]{2,1,0:T(8,128)(2,1)} %copy-done.12, bf16[8,16,512]{2,1,0:T(8,128)(2,1)} %copy-done.13, bf16[16,16,512]{2,1,0:T(8,128)(2,1)} %copy-done.3), custom_call_target="tpu_custom_call" | custom-call | tf_op jit(solution)/shard_map/place/pallas_call | solution.py:422
  (35 shorter events, 0.1 us)
Async XLA Ops:
  0.6 11.8 %collective-permute-start = (bf16[128,64,128]{2,1,0:T(8,128)(2,1)}, bf16[128,64,128]{2,1,0:T(8,128)(2,1)S(1)}, u32[]{:S(2)}, u32[]{:S(2)}) collective-permute-start(bf16[128,64,128]{2,1,0:T(8,128)(2,1)} %bitcast.10), channel_id=1, source_target_pairs={{0,1},{1,0},{2,3},{3,2},{4,5},{5,4},{6,7},{7,6},{8,9},{9,8},{10,11... | collective-permute-start | bytes 6291464 | tf_op jit(solution)/shard_map/ppermute | solution.py:447
  0.7 12.7 %collective-permute-start.1 = (bf16[128,64,128]{2,1,0:T(8,128)(2,1)}, bf16[128,64,128]{2,1,0:T(8,128)(2,1)}, u32[]{:S(2)}, u32[]{:S(2)}) collective-permute-start(bf16[128,64,128]{2,1,0:T(8,128)(2,1)} %bitcast.13), channel_id=1, source_target_pairs={{0,1},{1,0},{2,3},{3,2},{4,5},{5,4},{6,7},{7,6},{8,9},{9,8},{10,11... | collective-permute-start | bytes 6291464 | tf_op jit(solution)/shard_map/ppermute | solution.py:448
  5.9 53.8 %collective-permute-start.2 = (bf16[64,64,128]{2,1,0:T(8,128)(2,1)}, bf16[64,64,128]{2,1,0:T(8,128)(2,1)S(1)}, u32[]{:S(2)}, u32[]{:S(2)}) collective-permute-start(bf16[64,64,128]{2,1,0:T(8,128)(2,1)} %get-tuple-element.64), channel_id=1, source_target_pairs={{16,0},{32,16},{48,32},{0,48},{80,64},{96,80},{112,96},{64,112},{1... | collective-permute-start | bytes 3145736 | tf_op jit(solution)/shard_map/ppermute | solution.py:135
  8.9 53.2 %collective-permute-start.8 = (bf16[64,64,128]{2,1,0:T(8,128)(2,1)}, bf16[64,64,128]{2,1,0:T(8,128)(2,1)}, u32[]{:S(2)}, u32[]{:S(2)}) collective-permute-start(bf16[64,64,128]{2,1,0:T(8,128)(2,1)} %get-tuple-element.74), channel_id=1, source_target_pairs={{0,64},{16,80},{32,96},{48,112},{64,0},{80,16},{96,32},{112,48},{1... | collective-permute-start | bytes 3145736 | tf_op jit(solution)/shard_map/ppermute | solution.py:139
  12.1 45.4 %collective-permute-start.9 = (bf16[32,64,128]{2,1,0:T(8,128)(2,1)}, bf16[32,64,128]{2,1,0:T(8,128)(2,1)}, u32[]{:S(2)}, u32[]{:S(2)}) collective-permute-start(bf16[32,64,128]{2,1,0:T(8,128)(2,1)} %get-tuple-element.76), channel_id=1, source_target_pairs={{0,64},{16,80},{32,96},{48,112},{64,0},{80,16},{96,32},{112,48},{1... | collective-permute-start | bytes 1572872 | tf_op jit(solution)/shard_map/ppermute | solution.py:139
  12.4 4.5 %copy-start.1 = (bf16[128,64,128]{2,1,0:T(8,128)(2,1)}, bf16[128,64,128]{2,1,0:T(8,128)(2,1)S(1)}, u32[]{:S(2)}) copy-start(bf16[128,64,128]{2,1,0:T(8,128)(2,1)S(1)} %collective-permute-done.ok) | copy-start | bytes 6291460
  12.4 62.3 %collective-permute-start.3 = (bf16[64,64,128]{2,1,0:T(8,128)(2,1)}, bf16[64,64,128]{2,1,0:T(8,128)(2,1)}, u32[]{:S(2)}, u32[]{:S(2)}) collective-permute-start(bf16[64,64,128]{2,1,0:T(8,128)(2,1)} %get-tuple-element.66), channel_id=1, source_target_pairs={{0,16},{16,32},{32,48},{48,0},{64,80},{80,96},{96,112},{112,64},{1... | collective-permute-start | bytes 3145736 | tf_op jit(solution)/shard_map/ppermute | solution.py:129
  13.4 82.2 %collective-permute-start.7 = (bf16[32,64,128]{2,1,0:T(8,128)(2,1)}, bf16[32,64,128]{2,1,0:T(8,128)(2,1)}, u32[]{:S(2)}, u32[]{:S(2)}) collective-permute-start(bf16[32,64,128]{2,1,0:T(8,128)(2,1)} %get-tuple-element.72), channel_id=1, source_target_pairs={{0,64},{16,80},{32,96},{48,112},{64,0},{80,16},{96,32},{112,48},{1... | collective-permute-start | bytes 1572872 | tf_op jit(solution)/shard_map/ppermute | solution.py:139
  22.4 39.6 %copy-start.10 = (bf16[32,64,128]{2,1,0:T(8,128)(2,1)S(1)}, bf16[32,64,128]{2,1,0:T(8,128)(2,1)}, u32[]{:S(2)}) copy-start(bf16[32,64,128]{2,1,0:T(8,128)(2,1)} %get-tuple-element.68) | copy-start | bytes 1572868
  22.4 57.8 %all-to-all-start = ((bf16[8,576,128]{2,1,0:T(8,128)(2,1)}), bf16[8,576,128]{2,1,0:T(8,128)(2,1)S(1)}, u32[]{:S(2)}, u32[]{:S(2)}) async-start(bf16[8,576,128]{2,1,0:T(8,128)(2,1)} %attend.1), calls=%async_computation | async-start | bytes 2359296 | tf_op jit(solution)/shard_map/all_to_all | solution.py:433
  30.7 38.2 %copy-start.8 = (bf16[32,64,128]{2,1,0:T(8,128)(2,1)S(1)}, bf16[32,64,128]{2,1,0:T(8,128)(2,1)}, u32[]{:S(2)}) copy-start(bf16[32,64,128]{2,1,0:T(8,128)(2,1)} %get-tuple-element.73) | copy-start | bytes 1572868
  30.7 38.2 %copy-start.9 = (bf16[32,64,128]{2,1,0:T(8,128)(2,1)S(1)}, bf16[32,64,128]{2,1,0:T(8,128)(2,1)}, u32[]{:S(2)}) copy-start(bf16[32,64,128]{2,1,0:T(8,128)(2,1)} %get-tuple-element.77) | copy-start | bytes 1572868
  58.7 7.7 %collective-permute-start.10 = (bf16[16,64,128]{2,1,0:T(8,128)(2,1)S(1)}, bf16[16,64,128]{2,1,0:T(8,128)(2,1)S(1)}, u32[]{:S(2)}, u32[]{:S(2)}) collective-permute-start(bf16[16,64,128]{2,1,0:T(8,128)(2,1)S(1)} %get-tuple-element.84), channel_id=1, source_target_pairs={{0,16},{16,32},{32,48},{48,0},{64,80},{80,96},{96,112},{112,64},{1... | collective-permute-start | bytes 786440 | tf_op jit(solution)/shard_map/ppermute | solution.py:129
  59.7 9.2 %collective-permute-start.12 = (bf16[16,64,128]{2,1,0:T(8,128)(2,1)S(1)}, bf16[16,64,128]{2,1,0:T(8,128)(2,1)S(1)}, u32[]{:S(2)}, u32[]{:S(2)}) collective-permute-start(bf16[16,64,128]{2,1,0:T(8,128)(2,1)S(1)} %get-tuple-element.85), channel_id=1, source_target_pairs={{16,0},{32,16},{48,32},{0,48},{80,64},{96,80},{112,96},{64,112},{1... | collective-permute-start | bytes 786440 | tf_op jit(solution)/shard_map/ppermute | solution.py:135
  62.0 12.7 %copy-start.7 = (bf16[32,64,128]{2,1,0:T(8,128)(2,1)S(1)}, bf16[32,64,128]{2,1,0:T(8,128)(2,1)}, u32[]{:S(2)}) copy-start(bf16[32,64,128]{2,1,0:T(8,128)(2,1)} %get-tuple-element.65) | copy-start | bytes 1572868
  62.1 18.1 %collective-permute-start.5 = (bf16[32,64,128]{2,1,0:T(8,128)(2,1)S(1)}, bf16[32,64,128]{2,1,0:T(8,128)(2,1)}, u32[]{:S(2)}, u32[]{:S(2)}) collective-permute-start(bf16[32,64,128]{2,1,0:T(8,128)(2,1)S(1)} %slice_add_fusion.2), channel_id=1, source_target_pairs={{16,0},{32,16},{48,32},{0,48},{80,64},{96,80},{112,96},{64,112},{1... | collective-permute-start | bytes 1572872 | tf_op jit(solution)/shard_map/ppermute | solution.py:135
  71.2 24.6 %collective-permute-start.11 = (bf16[32,64,128]{2,1,0:T(8,128)(2,1)}, bf16[32,64,128]{2,1,0:T(8,128)(2,1)}, u32[]{:S(2)}, u32[]{:S(2)}) collective-permute-start(bf16[32,64,128]{2,1,0:T(8,128)(2,1)} %get-tuple-element.82), channel_id=1, source_target_pairs={{0,16},{16,32},{32,48},{48,0},{64,80},{80,96},{96,112},{112,64},{1... | collective-permute-start | bytes 1572872 | tf_op jit(solution)/shard_map/ppermute | solution.py:129
  73.1 25.9 %collective-permute-start.13 = (bf16[32,64,128]{2,1,0:T(8,128)(2,1)}, bf16[32,64,128]{2,1,0:T(8,128)(2,1)}, u32[]{:S(2)}, u32[]{:S(2)}) collective-permute-start(bf16[32,64,128]{2,1,0:T(8,128)(2,1)} %get-tuple-element.83), channel_id=1, source_target_pairs={{16,0},{32,16},{48,32},{0,48},{80,64},{96,80},{112,96},{64,112},{1... | collective-permute-start | bytes 1572872 | tf_op jit(solution)/shard_map/ppermute | solution.py:135
  76.6 22.4 %copy-start.6 = (bf16[32,64,128]{2,1,0:T(8,128)(2,1)S(1)}, bf16[32,64,128]{2,1,0:T(8,128)(2,1)}, u32[]{:S(2)}) copy-start(bf16[32,64,128]{2,1,0:T(8,128)(2,1)} %get-tuple-element.71) | copy-start | bytes 1572868
  76.6 30.1 %collective-permute-start.4 = (bf16[32,64,128]{2,1,0:T(8,128)(2,1)}, bf16[32,64,128]{2,1,0:T(8,128)(2,1)}, u32[]{:S(2)}, u32[]{:S(2)}) collective-permute-start(bf16[32,64,128]{2,1,0:T(8,128)(2,1)} %slice_add_fusion.3), channel_id=1, source_target_pairs={{0,16},{16,32},{32,48},{48,0},{64,80},{80,96},{96,112},{112,64},{1... | collective-permute-start | bytes 1572872 | tf_op jit(solution)/shard_map/ppermute | solution.py:129
  80.2 1.0 copy-start
  84.0 11.6 %copy-start.11 = (bf16[8,16,512]{2,1,0:T(8,128)(2,1)S(1)}, bf16[8,16,512]{2,1,0:T(8,128)(2,1)}, u32[]{:S(2)}) copy-start(bf16[8,16,512]{2,1,0:T(8,128)(2,1)} %join.1) | copy-start | bytes 393220
  84.0 8.2 %collective-permute-start.14 = (bf16[8,16,512]{2,1,0:T(8,128)(2,1)}, bf16[8,16,512]{2,1,0:T(8,128)(2,1)S(1)}, u32[]{:S(2)}, u32[]{:S(2)}) collective-permute-start(bf16[8,16,512]{2,1,0:T(8,128)(2,1)} %join.1), channel_id=1, source_target_pairs={{0,64},{16,80},{32,96},{48,112},{64,0},{80,16},{96,32},{112,48},{1... | collective-permute-start | bytes 393224 | tf_op jit(solution)/shard_map/ppermute | solution.py:139
  89.0 17.8 %copy-start.5 = (bf16[32,64,128]{2,1,0:T(8,128)(2,1)S(1)}, bf16[32,64,128]{2,1,0:T(8,128)(2,1)}, u32[]{:S(2)}) copy-start(bf16[32,64,128]{2,1,0:T(8,128)(2,1)} %get-tuple-element.63) | copy-start | bytes 1572868
  92.2 14.6 %collective-permute-start.6 = (bf16[32,64,128]{2,1,0:T(8,128)(2,1)S(1)}, bf16[32,64,128]{2,1,0:T(8,128)(2,1)S(1)}, u32[]{:S(2)}, u32[]{:S(2)}) collective-permute-start(bf16[32,64,128]{2,1,0:T(8,128)(2,1)S(1)} %add_add_fusion), channel_id=1, source_target_pairs={{0,64},{16,80},{32,96},{48,112},{64,0},{80,16},{96,32},{112,48},{1... | collective-permute-start | bytes 1572872 | tf_op jit(solution)/shard_map/ppermute | solution.py:139
  95.7 13.0 %copy-start.2 = (bf16[16,16,512]{2,1,0:T(8,128)(2,1)}, bf16[16,16,512]{2,1,0:T(8,128)(2,1)S(1)}, u32[]{:S(2)}) copy-start(bf16[16,16,512]{2,1,0:T(8,128)(2,1)S(1)} %pad_maximum_fusion.pair) | copy-start | bytes 786436
  95.7 7.7 %collective-permute-start.16 = (bf16[16,16,512]{2,1,0:T(8,128)(2,1)S(1)}, bf16[16,16,512]{2,1,0:T(8,128)(2,1)S(1)}, u32[]{:S(2)}, u32[]{:S(2)}) collective-permute-start(bf16[16,16,512]{2,1,0:T(8,128)(2,1)S(1)} %pad_maximum_fusion.pair), channel_id=1, source_target_pairs={{0,16},{16,32},{32,48},{48,0},{64,80},{80,96},{96,112},{112,64},{1... | collective-permute-start | bytes 786440 | tf_op jit(solution)/shard_map/ppermute | solution.py:129
  95.8 7.6 %collective-permute-start.15 = (bf16[16,16,512]{2,1,0:T(8,128)(2,1)S(1)}, bf16[16,16,512]{2,1,0:T(8,128)(2,1)S(1)}, u32[]{:S(2)}, u32[]{:S(2)}) collective-permute-start(bf16[16,16,512]{2,1,0:T(8,128)(2,1)S(1)} %pad_maximum_fusion.pair), channel_id=1, source_target_pairs={{16,0},{32,16},{48,32},{0,48},{80,64},{96,80},{112,96},{64,112},{1... | collective-permute-start | bytes 786440 | tf_op jit(solution)/shard_map/ppermute | solution.py:135
  103.3 6.3 %copy-start.3 = (bf16[16,16,512]{2,1,0:T(8,128)(2,1)}, bf16[16,16,512]{2,1,0:T(8,128)(2,1)S(1)}, u32[]{:S(2)}) copy-start(bf16[16,16,512]{2,1,0:T(8,128)(2,1)S(1)} %collective-permute-done.16.west) | copy-start | bytes 786436
  103.3 6.2 %collective-permute-start.17 = (bf16[8,16,512]{2,1,0:T(8,128)(2,1)S(1)}, bf16[8,16,512]{2,1,0:T(8,128)(2,1)S(1)}, u32[]{:S(2)}, u32[]{:S(2)}) collective-permute-start(bf16[8,16,512]{2,1,0:T(8,128)(2,1)S(1)} %slice.55), channel_id=1, source_target_pairs={{0,16},{16,32},{32,48},{48,0},{64,80},{80,96},{96,112},{112,64},{1... | collective-permute-start | bytes 393224 | tf_op jit(solution)/shard_map/ppermute | solution.py:129
  103.4 6.2 %copy-start.4 = (bf16[16,16,512]{2,1,0:T(8,128)(2,1)}, bf16[16,16,512]{2,1,0:T(8,128)(2,1)S(1)}, u32[]{:S(2)}) copy-start(bf16[16,16,512]{2,1,0:T(8,128)(2,1)S(1)} %collective-permute-done.15.east) | copy-start | bytes 786436
  103.5 6.1 %collective-permute-start.18 = (bf16[8,16,512]{2,1,0:T(8,128)(2,1)S(1)}, bf16[8,16,512]{2,1,0:T(8,128)(2,1)S(1)}, u32[]{:S(2)}, u32[]{:S(2)}) collective-permute-start(bf16[8,16,512]{2,1,0:T(8,128)(2,1)S(1)} %slice.56), channel_id=1, source_target_pairs={{16,0},{32,16},{48,32},{0,48},{80,64},{96,80},{112,96},{64,112},{1... | collective-permute-start | bytes 393224 | tf_op jit(solution)/shard_map/ppermute | solution.py:135
  109.6 0.6 copy-start.12
  110.2 0.7 copy-start.13

commit v2 on v0

--- a/solution.py
+++ b/solution.py
@@ -316,7 +316,7 @@
     lax.fori_loop(0, insts, finish, 0)
 
 
-UNROLL = 16
+UNROLL = 32
 SETTLE = 16
 
 
@@ -414,14 +414,16 @@
     other_v = lax.ppermute(values, "head", swap)
 
     table = table_of(blocks // insts, rows, half, head_dim)
-    out_k, out_v = pack(old_block, new_slot, table, keys, values, insts, SENT_K, SENT_V)
+    out_k, out_v = pack(
+        old_block, new_slot, table, keys, values, insts, SENT_K + KEPT_K, SENT_V + KEPT_V
+    )
     queries, out_k, out_v = lax.optimization_barrier((queries, out_k, out_v))
     shape = (blocks // insts, entries, half, head_dim)
     far2 = across(out_v[0])
     from_left = right(out_k[0])
     from_right = left(out_k[1])
     far = across(out_v[1])
-    kept_k, kept_v = pack(old_block, new_slot, table, keys, values, insts, KEPT_K, KEPT_V)
+    kept_k, kept_v = out_k[len(SENT_K) :], out_v[len(SENT_V) :]
     near = across(kept_v[0])
     packet = attend(
         old_block, lengths, table, queries, keys, values, other_k, other_v,

time: 114 us -> 115 us (level)
  waiting for transfers between devices: 42.7 us -> 48.9 us
  starting transfers between devices: 41.4 us -> 38.4 us
  Pallas kernels: 14.3 us -> 12.8 us
    ppermute x4, waiting for transfers between devices: 33 us -> 39.1 us  [across(): lax.ppermute(x, 'inst', [(i, i ^ COLS) for i in range(lax.axis_size('inst...]
    ppermute x4, starting transfers between devices: 12.7 us -> 10.6 us  [across(): lax.ppermute(x, 'inst', [(i, i ^ COLS) for i in range(lax.axis_size('inst...]
    pallas_call x2 -> x1, Pallas kernels: 5.69 us -> 4.18 us  [pack(): pl.pallas_call(functools.partial(pack_body, groups_k, groups_v), in_specs...]
  transfers between devices with their start and end apart: 16 -> 16, of which waited for: 5 -> 5; matrix products, arithmetic and copies ran while one was open for 10% -> 10% of each run, Pallas kernels for 13% -> 11%
where the time goes in v2:
time: 115 us
  waiting for transfers between devices  48.9 us (43%)
  starting transfers between devices  38.4 us (33%)
  Pallas kernels  12.8 us (11%)
  other arithmetic  11.8 us (10%)
  local copies, waits for them, and re-layouts  2.05 us (2%)
    ppermute x4, waiting for transfers between devices, across(): lax.ppermute(x, 'inst', [(i, i ^ COLS) for i in range(lax.axis_size('inst...  39.1 us
    all_to_all x2, starting transfers between devices, spread(): return lax.all_to_all(x, 'inst', split_axis=0, concat_axis=0, tiled=True)  15.8 us
    ppermute x4, starting transfers between devices, across(): lax.ppermute(x, 'inst', [(i, i ^ COLS) for i in range(lax.axis_size('inst...  10.6 us
    ppermute x4, starting transfers between devices, left(): return lax.ppermute(x, 'inst', route)  7.2 us
    ppermute x4, waiting for transfers between devices, left(): return lax.ppermute(x, 'inst', route)  5.8 us
    pallas_call x1, Pallas kernels, attend(): pl.pallas_call(attend_body, in_specs=[smem] * 3 + [anyspace] * 7, out_spe...  5.51 us
    ppermute x4, starting transfers between devices, right(): return lax.ppermute(x, 'inst', route)  4.22 us
    unnamed x2, other arithmetic  4.19 us
  transfers between devices with their start and end apart: 16, of which 5 were waited for; matrix products, arithmetic and copies ran while one was open for 10% of the time, Pallas kernels for 11%

profile of v2, /device:TPU:0, one launch (start us, length us, event | category | flops | bytes accessed | tf_op | source)
XLA Modules:
  0.0 114.6 jit_solution(16556654915946092888)
XLA Ops:
  0.6 0.1 collective-permute-start
  0.7 0.5 collective-permute-start.1
  1.2 0.6 compare_select_fusion.4.base.meta
  1.8 4.2 %shard_map.103 = (bf16[64,64,128]{2,1,0:T(8,128)(2,1)}, bf16[64,64,128]{2,1,0:T(8,128)(2,1)}, bf16[32,64,128]{2,1,0:T(8,128)(2,1)}, bf16[32,64,128]{2,1,0:T(8,12...) custom-call(s32[128]{0:T(128)} %old_block.3, ...), custom_call_target="tpu_custom_call" | custom-call | tf_op jit(solution)/shard_map/pallas_call | solution.py:107
  6.0 2.9 %collective-permute-start.2 = (bf16[64,64,128]{2,1,0:T(8,128)(2,1)}, bf16[64,64,128]{2,1,0:T(8,128)(2,1)S(1)}, u32[]{:S(2)}, u32[]{:S(2)}) collective-permute-start(bf16[64,64,128]{2,1,0:T(8,128)(2,1)} %get-tuple-element.64), channel_id=1, source_target_pairs={{16,0},{32,16},{48,32},{0,48},{80,64},{96,80},{112,96},{64,112},{1... | collective-permute-start | bytes 3145736 | tf_op jit(solution)/shard_map/ppermute | solution.py:135
  8.9 3.2 %collective-permute-start.8 = (bf16[64,64,128]{2,1,0:T(8,128)(2,1)}, bf16[64,64,128]{2,1,0:T(8,128)(2,1)}, u32[]{:S(2)}, u32[]{:S(2)}) collective-permute-start(bf16[64,64,128]{2,1,0:T(8,128)(2,1)} %get-tuple-element.74), channel_id=1, source_target_pairs={{0,64},{16,80},{32,96},{48,112},{64,0},{80,16},{96,32},{112,48},{1... | collective-permute-start | bytes 3145736 | tf_op jit(solution)/shard_map/ppermute | solution.py:139
  12.1 0.3 collective-permute-start.9
  12.5 0.0 collective-permute-done.ok
  12.5 1.0 collective-permute-start.3
  13.5 0.0 collective-permute-done.1.ov
  13.5 3.5 %collective-permute-start.7 = (bf16[32,64,128]{2,1,0:T(8,128)(2,1)}, bf16[32,64,128]{2,1,0:T(8,128)(2,1)}, u32[]{:S(2)}, u32[]{:S(2)}) collective-permute-start(bf16[32,64,128]{2,1,0:T(8,128)(2,1)} %get-tuple-element.72), channel_id=1, source_target_pairs={{0,64},{16,80},{32,96},{48,112},{64,0},{80,16},{96,32},{112,48},{1... | collective-permute-start | bytes 1572872 | tf_op jit(solution)/shard_map/ppermute | solution.py:139
  17.0 0.0 copy-done.1
  17.0 5.5 %attend.1 = bf16[8,576,128]{2,1,0:T(8,128)(2,1)} custom-call(s32[128]{0:T(128)} %old_block.3, s32[64]{0:T(128)} %lengths.1, s32[16]{0:T(128)} %compare_select_fusion.4.base.meta, bf16[64,16,512]{2,1,0:T(8,128)(2,1)} %q, bf16[128,64,128]{2,1,0:T(8,128)(2,1)} %bitcast.13, bf16[128,64,128]{2,1,0:T(8,128)(2,1)} %bitcast.16, bf16[128,64,128]{2,1,0:T(8,128)(2,1)} %copy-done.1, ...), custom_call_target="tpu_custom_call" | custom-call | tf_op jit(solution)/shard_map/attend/pallas_call | solution.py:333
  22.5 0.0 copy-start.7
  22.5 8.2 %all-to-all-start = ((bf16[8,576,128]{2,1,0:T(8,128)(2,1)}), bf16[8,576,128]{2,1,0:T(8,128)(2,1)S(1)}, u32[]{:S(2)}, u32[]{:S(2)}) async-start(bf16[8,576,128]{2,1,0:T(8,128)(2,1)} %attend.1), calls=%async_computation | async-start | bytes 2359296 | tf_op jit(solution)/shard_map/all_to_all | solution.py:399
  30.8 26.8 %collective-permute-done.9 = bf16[32,64,128]{2,1,0:T(8,128)(2,1)} collective-permute-done((bf16[32,64,128]{2,1,0:T(8,128)(2,1)}, bf16[32,64,128]{2,1,0:T(8,128)(2,1)}, u32[]{:S(2)}, u32[]{:S(2)}) %collective-permute-start.9) | collective-permute-done | bytes 524320 | tf_op jit(solution)/shard_map/ppermute | solution.py:139
  57.5 1.2 %slice_add_fusion.6 = (bf16[16,64,128]{2,1,0:T(8,128)(2,1)S(1)}, bf16[16,64,128]{2,1,0:T(8,128)(2,1)S(1)}) fusion(bf16[32,64,128]{2,1,0:T(8,128)(2,1)} %collective-permute-done.9, bf16[32,64,128]{2,1,0:T(8,128)(2,1)} %get-tuple-element.75), kind=kLoop, calls=%fused_computation.13 | loop fusion | flops 262144 | bytes 1572864 | tf_op jit(solution)/shard_map/add | solution.py:156
  58.7 1.0 collective-permute-start.10
  59.8 0.0 collective-permute-done.2
  59.8 2.3 %collective-permute-start.12 = (bf16[16,64,128]{2,1,0:T(8,128)(2,1)S(1)}, bf16[16,64,128]{2,1,0:T(8,128)(2,1)S(1)}, u32[]{:S(2)}, u32[]{:S(2)}) collective-permute-start(bf16[16,64,128]{2,1,0:T(8,128)(2,1)S(1)} %get-tuple-element.85), channel_id=1, source_target_pairs={{16,0},{32,16},{48,32},{0,48},{80,64},{96,80},{112,96},{64,112},{1... | collective-permute-start | bytes 786440 | tf_op jit(solution)/shard_map/ppermute | solution.py:135
  62.1 0.1 slice_add_fusion.2
  62.1 0.0 copy-start.4
  62.1 0.0 collective-permute-done.8
  62.1 0.3 collective-permute-start.5
  62.4 4.0 %collective-permute-done.10 = bf16[16,64,128]{2,1,0:T(8,128)(2,1)S(1)} collective-permute-done((bf16[16,64,128]{2,1,0:T(8,128)(2,1)S(1)}, bf16[16,64,128]{2,1,0:T(8,128)(2,1)S(1)}, u32[]{:S(2)}, u32[]{:S(2)}) %collective-permute-start.10) | collective-permute-done | bytes 262176 | tf_op jit(solution)/shard_map/ppermute | solution.py:129
  66.4 2.5 %collective-permute-done.12 = bf16[16,64,128]{2,1,0:T(8,128)(2,1)S(1)} collective-permute-done((bf16[16,64,128]{2,1,0:T(8,128)(2,1)S(1)}, bf16[16,64,128]{2,1,0:T(8,128)(2,1)S(1)}, u32[]{:S(2)}, u32[]{:S(2)}) %collective-permute-start.12) | collective-permute-done | bytes 262176 | tf_op jit(solution)/shard_map/ppermute | solution.py:135
  69.0 2.3 %fusion.1 = (bf16[32,64,128]{2,1,0:T(8,128)(2,1)}, bf16[32,64,128]{2,1,0:T(8,128)(2,1)}) fusion(bf16[32,64,128]{2,1,0:T(8,128)(2,1)S(1)} %copy-done.5, bf16[64,64,128]{2,1,0:T(8,128)(2,1)} %collective-permute-done.8, bf16[16,64,128]{2,1,0:T(8,128)(2,1)S(1)} %collective-permute-done.10, bf16[16,64,128]{2,1,0:T(8,128)(2,1)S(1)} %collective-permute-done.12, ...), kind=kLoop, calls=%fused_computation.3 | loop fusion | flops 1048576 | bytes 3670016 | tf_op jit(solution)/shard_map/add | solution.py:159
  71.3 1.8 %collective-permute-start.11 = (bf16[32,64,128]{2,1,0:T(8,128)(2,1)}, bf16[32,64,128]{2,1,0:T(8,128)(2,1)}, u32[]{:S(2)}, u32[]{:S(2)}) collective-permute-start(bf16[32,64,128]{2,1,0:T(8,128)(2,1)} %get-tuple-element.82), channel_id=1, source_target_pairs={{0,16},{16,32},{32,48},{48,0},{64,80},{80,96},{96,112},{112,64},{1... | collective-permute-start | bytes 1572872 | tf_op jit(solution)/shard_map/ppermute | solution.py:129
  73.1 1.7 %collective-permute-start.13 = (bf16[32,64,128]{2,1,0:T(8,128)(2,1)}, bf16[32,64,128]{2,1,0:T(8,128)(2,1)}, u32[]{:S(2)}, u32[]{:S(2)}) collective-permute-start(bf16[32,64,128]{2,1,0:T(8,128)(2,1)} %get-tuple-element.83), channel_id=1, source_target_pairs={{16,0},{32,16},{48,32},{0,48},{80,64},{96,80},{112,96},{64,112},{1... | collective-permute-start | bytes 1572872 | tf_op jit(solution)/shard_map/ppermute | solution.py:135
  74.8 0.0 collective-permute-done.3
  74.8 1.9 %slice_add_fusion.3 = bf16[32,64,128]{2,1,0:T(8,128)(2,1)} fusion(bf16[32,64,128]{2,1,0:T(8,128)(2,1)S(1)} %copy-done.4, bf16[64,64,128]{2,1,0:T(8,128)(2,1)} %collective-permute-done.3), kind=kLoop, calls=%fused_computation.5 | loop fusion | flops 262144 | bytes 1572864 | tf_op jit(solution)/shard_map/add | solution.py:145
  76.7 0.4 collective-permute-start.4
  77.0 3.2 %collective-permute-done.5 = bf16[32,64,128]{2,1,0:T(8,128)(2,1)} collective-permute-done((bf16[32,64,128]{2,1,0:T(8,128)(2,1)S(1)}, bf16[32,64,128]{2,1,0:T(8,128)(2,1)}, u32[]{:S(2)}, u32[]{:S(2)}) %collective-permute-start.5) | collective-permute-done | bytes 524320 | tf_op jit(solution)/shard_map/ppermute | solution.py:135
  80.3 0.0 all-to-all-done.got
  80.3 1.0 copy-done
  81.3 3.1 %join.1 = bf16[8,8,16,512]{3,2,1,0:T(8,128)(2,1)} custom-call(bf16[8,576,128]{2,1,0:T(8,128)(2,1)} %copy-done), custom_call_target="tpu_custom_call" | custom-call | tf_op jit(solution)/shard_map/join/pallas_call | solution.py:389
  84.4 7.5 %all-to-all-start.1 = ((bf16[8,8,16,512]{3,2,1,0:T(8,128)(2,1)}), bf16[8,8,16,512]{3,2,1,0:T(8,128)(2,1)S(1)}, u32[]{:S(2)}, u32[]{:S(2)}) async-start(bf16[8,8,16,512]{3,2,1,0:T(8,128)(2,1)} %join.1), calls=%async_computation.1 | async-start | bytes 2097152 | tf_op jit(solution)/shard_map/all_to_all | solution.py:399
  92.0 1.5 %add_add_fusion = bf16[32,64,128]{2,1,0:T(8,128)(2,1)S(1)} fusion(bf16[32,64,128]{2,1,0:T(8,128)(2,1)} %collective-permute-done.5, bf16[32,64,128]{2,1,0:T(8,128)(2,1)} %get-tuple-element.67, bf16[64,64,128]{2,1,0:T(8,128)(2,1)} %collective-permute-done.3), kind=kLoop, calls=%fused_computation.11 | loop fusion | flops 524288 | bytes 2097152 | tf_op jit(solution)/shard_map/add | solution.py:148
  93.5 3.6 %collective-permute-start.6 = (bf16[32,64,128]{2,1,0:T(8,128)(2,1)S(1)}, bf16[32,64,128]{2,1,0:T(8,128)(2,1)S(1)}, u32[]{:S(2)}, u32[]{:S(2)}) collective-permute-start(bf16[32,64,128]{2,1,0:T(8,128)(2,1)S(1)} %add_add_fusion), channel_id=1, source_target_pairs={{0,64},{16,80},{32,96},{48,112},{64,0},{80,16},{96,32},{112,48},{1... | collective-permute-start | bytes 1572872 | tf_op jit(solution)/shard_map/ppermute | solution.py:139
  97.1 0.0 collective-permute-done.7
  97.1 0.0 collective-permute-done.11
  97.1 0.0 collective-permute-done.13
  97.1 2.3 %add_bitcast_fusion = bf16[32,1,64,128]{3,2,1,0:T(8,128)(2,1)} fusion(bf16[32,64,128]{2,1,0:T(8,128)(2,1)} %collective-permute-done.13, bf16[32,64,128]{2,1,0:T(8,128)(2,1)} %collective-permute-done.11, bf16[32,64,128]{2,1,0:T(8,128)(2,1)S(1)} %copy-done.3, bf16[32,64,128]{2,1,0:T(8,128)(2,1)} %collective-permute-done.7), kind=kLoop, calls=%fused_computation.10 | loop fusion | flops 786432 | bytes 2621440
  99.3 0.0 collective-permute-done.4
  99.3 12.3 %collective-permute-done.6 = bf16[32,64,128]{2,1,0:T(8,128)(2,1)S(1)} collective-permute-done((bf16[32,64,128]{2,1,0:T(8,128)(2,1)S(1)}, bf16[32,64,128]{2,1,0:T(8,128)(2,1)S(1)}, u32[]{:S(2)}, u32[]{:S(2)}) %collective-permute-start.6) | collective-permute-done | bytes 524320 | tf_op jit(solution)/shard_map/ppermute | solution.py:139
  111.7 1.9 %fusion.4 = bf16[32,1,64,128]{3,2,1,0:T(8,128)(2,1)} fusion(bf16[32,64,128]{2,1,0:T(8,128)(2,1)S(1)} %collective-permute-done.6, bf16[32,64,128]{2,1,0:T(8,128)(2,1)} %collective-permute-done.4, bf16[32,64,128]{2,1,0:T(8,128)(2,1)S(1)} %copy-done.2, bf16[64,64,128]{2,1,0:T(8,128)(2,1)S(1)} %collective-permute-done.2), kind=kLoop, calls=%fused_computation.9 | loop fusion | flops 786432 | bytes 2621440
  113.6 0.0 all-to-all-done.1
  113.6 1.0 copy.14
  (12 shorter events, 0.0 us)
Async XLA Ops:
  0.6 11.8 %collective-permute-start = (bf16[128,64,128]{2,1,0:T(8,128)(2,1)}, bf16[128,64,128]{2,1,0:T(8,128)(2,1)S(1)}, u32[]{:S(2)}, u32[]{:S(2)}) collective-permute-start(bf16[128,64,128]{2,1,0:T(8,128)(2,1)} %bitcast.11), channel_id=1, source_target_pairs={{0,1},{1,0},{2,3},{3,2},{4,5},{5,4},{6,7},{7,6},{8,9},{9,8},{10,11... | collective-permute-start | bytes 6291464 | tf_op jit(solution)/shard_map/ppermute | solution.py:413
  0.7 12.8 %collective-permute-start.1 = (bf16[128,64,128]{2,1,0:T(8,128)(2,1)}, bf16[128,64,128]{2,1,0:T(8,128)(2,1)}, u32[]{:S(2)}, u32[]{:S(2)}) collective-permute-start(bf16[128,64,128]{2,1,0:T(8,128)(2,1)} %bitcast.14), channel_id=1, source_target_pairs={{0,1},{1,0},{2,3},{3,2},{4,5},{5,4},{6,7},{7,6},{8,9},{9,8},{10,11... | collective-permute-start | bytes 6291464 | tf_op jit(solution)/shard_map/ppermute | solution.py:414
  6.0 53.8 %collective-permute-start.2 = (bf16[64,64,128]{2,1,0:T(8,128)(2,1)}, bf16[64,64,128]{2,1,0:T(8,128)(2,1)S(1)}, u32[]{:S(2)}, u32[]{:S(2)}) collective-permute-start(bf16[64,64,128]{2,1,0:T(8,128)(2,1)} %get-tuple-element.64), channel_id=1, source_target_pairs={{16,0},{32,16},{48,32},{0,48},{80,64},{96,80},{112,96},{64,112},{1... | collective-permute-start | bytes 3145736 | tf_op jit(solution)/shard_map/ppermute | solution.py:135
  8.9 53.2 %collective-permute-start.8 = (bf16[64,64,128]{2,1,0:T(8,128)(2,1)}, bf16[64,64,128]{2,1,0:T(8,128)(2,1)}, u32[]{:S(2)}, u32[]{:S(2)}) collective-permute-start(bf16[64,64,128]{2,1,0:T(8,128)(2,1)} %get-tuple-element.74), channel_id=1, source_target_pairs={{0,64},{16,80},{32,96},{48,112},{64,0},{80,16},{96,32},{112,48},{1... | collective-permute-start | bytes 3145736 | tf_op jit(solution)/shard_map/ppermute | solution.py:139
  12.1 45.4 %collective-permute-start.9 = (bf16[32,64,128]{2,1,0:T(8,128)(2,1)}, bf16[32,64,128]{2,1,0:T(8,128)(2,1)}, u32[]{:S(2)}, u32[]{:S(2)}) collective-permute-start(bf16[32,64,128]{2,1,0:T(8,128)(2,1)} %get-tuple-element.76), channel_id=1, source_target_pairs={{0,64},{16,80},{32,96},{48,112},{64,0},{80,16},{96,32},{112,48},{1... | collective-permute-start | bytes 1572872 | tf_op jit(solution)/shard_map/ppermute | solution.py:139
  12.5 4.5 %copy-start.1 = (bf16[128,64,128]{2,1,0:T(8,128)(2,1)}, bf16[128,64,128]{2,1,0:T(8,128)(2,1)S(1)}, u32[]{:S(2)}) copy-start(bf16[128,64,128]{2,1,0:T(8,128)(2,1)S(1)} %collective-permute-done.ok) | copy-start | bytes 6291460
  12.5 62.3 %collective-permute-start.3 = (bf16[64,64,128]{2,1,0:T(8,128)(2,1)}, bf16[64,64,128]{2,1,0:T(8,128)(2,1)}, u32[]{:S(2)}, u32[]{:S(2)}) collective-permute-start(bf16[64,64,128]{2,1,0:T(8,128)(2,1)} %get-tuple-element.66), channel_id=1, source_target_pairs={{0,16},{16,32},{32,48},{48,0},{64,80},{80,96},{96,112},{112,64},{1... | collective-permute-start | bytes 3145736 | tf_op jit(solution)/shard_map/ppermute | solution.py:129
  13.5 83.6 %collective-permute-start.7 = (bf16[32,64,128]{2,1,0:T(8,128)(2,1)}, bf16[32,64,128]{2,1,0:T(8,128)(2,1)}, u32[]{:S(2)}, u32[]{:S(2)}) collective-permute-start(bf16[32,64,128]{2,1,0:T(8,128)(2,1)} %get-tuple-element.72), channel_id=1, source_target_pairs={{0,64},{16,80},{32,96},{48,112},{64,0},{80,16},{96,32},{112,48},{1... | collective-permute-start | bytes 1572872 | tf_op jit(solution)/shard_map/ppermute | solution.py:139
  22.5 39.6 %copy-start.7 = (bf16[32,64,128]{2,1,0:T(8,128)(2,1)S(1)}, bf16[32,64,128]{2,1,0:T(8,128)(2,1)}, u32[]{:S(2)}) copy-start(bf16[32,64,128]{2,1,0:T(8,128)(2,1)} %get-tuple-element.68) | copy-start | bytes 1572868
  22.5 57.8 %all-to-all-start = ((bf16[8,576,128]{2,1,0:T(8,128)(2,1)}), bf16[8,576,128]{2,1,0:T(8,128)(2,1)S(1)}, u32[]{:S(2)}, u32[]{:S(2)}) async-start(bf16[8,576,128]{2,1,0:T(8,128)(2,1)} %attend.1), calls=%async_computation | async-start | bytes 2359296 | tf_op jit(solution)/shard_map/all_to_all | solution.py:399
  30.7 38.2 %copy-start.5 = (bf16[32,64,128]{2,1,0:T(8,128)(2,1)S(1)}, bf16[32,64,128]{2,1,0:T(8,128)(2,1)}, u32[]{:S(2)}) copy-start(bf16[32,64,128]{2,1,0:T(8,128)(2,1)} %get-tuple-element.73) | copy-start | bytes 1572868
  30.7 38.2 %copy-start.6 = (bf16[32,64,128]{2,1,0:T(8,128)(2,1)S(1)}, bf16[32,64,128]{2,1,0:T(8,128)(2,1)}, u32[]{:S(2)}) copy-start(bf16[32,64,128]{2,1,0:T(8,128)(2,1)} %get-tuple-element.77) | copy-start | bytes 1572868
  58.7 7.7 %collective-permute-start.10 = (bf16[16,64,128]{2,1,0:T(8,128)(2,1)S(1)}, bf16[16,64,128]{2,1,0:T(8,128)(2,1)S(1)}, u32[]{:S(2)}, u32[]{:S(2)}) collective-permute-start(bf16[16,64,128]{2,1,0:T(8,128)(2,1)S(1)} %get-tuple-element.84), channel_id=1, source_target_pairs={{0,16},{16,32},{32,48},{48,0},{64,80},{80,96},{96,112},{112,64},{1... | collective-permute-start | bytes 786440 | tf_op jit(solution)/shard_map/ppermute | solution.py:129
  59.8 9.2 %collective-permute-start.12 = (bf16[16,64,128]{2,1,0:T(8,128)(2,1)S(1)}, bf16[16,64,128]{2,1,0:T(8,128)(2,1)S(1)}, u32[]{:S(2)}, u32[]{:S(2)}) collective-permute-start(bf16[16,64,128]{2,1,0:T(8,128)(2,1)S(1)} %get-tuple-element.85), channel_id=1, source_target_pairs={{16,0},{32,16},{48,32},{0,48},{80,64},{96,80},{112,96},{64,112},{1... | collective-permute-start | bytes 786440 | tf_op jit(solution)/shard_map/ppermute | solution.py:135
  62.1 12.7 %copy-start.4 = (bf16[32,64,128]{2,1,0:T(8,128)(2,1)S(1)}, bf16[32,64,128]{2,1,0:T(8,128)(2,1)}, u32[]{:S(2)}) copy-start(bf16[32,64,128]{2,1,0:T(8,128)(2,1)} %get-tuple-element.65) | copy-start | bytes 1572868
  62.1 18.1 %collective-permute-start.5 = (bf16[32,64,128]{2,1,0:T(8,128)(2,1)S(1)}, bf16[32,64,128]{2,1,0:T(8,128)(2,1)}, u32[]{:S(2)}, u32[]{:S(2)}) collective-permute-start(bf16[32,64,128]{2,1,0:T(8,128)(2,1)S(1)} %slice_add_fusion.2), channel_id=1, source_target_pairs={{16,0},{32,16},{48,32},{0,48},{80,64},{96,80},{112,96},{64,112},{1... | collective-permute-start | bytes 1572872 | tf_op jit(solution)/shard_map/ppermute | solution.py:135
  71.3 25.8 %collective-permute-start.11 = (bf16[32,64,128]{2,1,0:T(8,128)(2,1)}, bf16[32,64,128]{2,1,0:T(8,128)(2,1)}, u32[]{:S(2)}, u32[]{:S(2)}) collective-permute-start(bf16[32,64,128]{2,1,0:T(8,128)(2,1)} %get-tuple-element.82), channel_id=1, source_target_pairs={{0,16},{16,32},{32,48},{48,0},{64,80},{80,96},{96,112},{112,64},{1... | collective-permute-start | bytes 1572872 | tf_op jit(solution)/shard_map/ppermute | solution.py:129
  73.1 23.9 %collective-permute-start.13 = (bf16[32,64,128]{2,1,0:T(8,128)(2,1)}, bf16[32,64,128]{2,1,0:T(8,128)(2,1)}, u32[]{:S(2)}, u32[]{:S(2)}) collective-permute-start(bf16[32,64,128]{2,1,0:T(8,128)(2,1)} %get-tuple-element.83), channel_id=1, source_target_pairs={{16,0},{32,16},{48,32},{0,48},{80,64},{96,80},{112,96},{64,112},{1... | collective-permute-start | bytes 1572872 | tf_op jit(solution)/shard_map/ppermute | solution.py:135
  76.7 22.6 %collective-permute-start.4 = (bf16[32,64,128]{2,1,0:T(8,128)(2,1)}, bf16[32,64,128]{2,1,0:T(8,128)(2,1)}, u32[]{:S(2)}, u32[]{:S(2)}) collective-permute-start(bf16[32,64,128]{2,1,0:T(8,128)(2,1)} %slice_add_fusion.3), channel_id=1, source_target_pairs={{0,16},{16,32},{32,48},{48,0},{64,80},{80,96},{96,112},{112,64},{1... | collective-permute-start | bytes 1572872 | tf_op jit(solution)/shard_map/ppermute | solution.py:129
  80.3 1.0 copy-start
  84.4 12.7 %copy-start.3 = (bf16[32,64,128]{2,1,0:T(8,128)(2,1)S(1)}, bf16[32,64,128]{2,1,0:T(8,128)(2,1)}, u32[]{:S(2)}) copy-start(bf16[32,64,128]{2,1,0:T(8,128)(2,1)} %get-tuple-element.71) | copy-start | bytes 1572868
  84.4 29.2 %all-to-all-start.1 = ((bf16[8,8,16,512]{3,2,1,0:T(8,128)(2,1)}), bf16[8,8,16,512]{3,2,1,0:T(8,128)(2,1)S(1)}, u32[]{:S(2)}, u32[]{:S(2)}) async-start(bf16[8,8,16,512]{3,2,1,0:T(8,128)(2,1)} %join.1), calls=%async_computation.1 | async-start | bytes 2097152 | tf_op jit(solution)/shard_map/all_to_all | solution.py:399
  92.0 19.7 %copy-start.2 = (bf16[32,64,128]{2,1,0:T(8,128)(2,1)S(1)}, bf16[32,64,128]{2,1,0:T(8,128)(2,1)}, u32[]{:S(2)}) copy-start(bf16[32,64,128]{2,1,0:T(8,128)(2,1)} %get-tuple-element.63) | copy-start | bytes 1572868
  93.5 18.2 %collective-permute-start.6 = (bf16[32,64,128]{2,1,0:T(8,128)(2,1)S(1)}, bf16[32,64,128]{2,1,0:T(8,128)(2,1)S(1)}, u32[]{:S(2)}, u32[]{:S(2)}) collective-permute-start(bf16[32,64,128]{2,1,0:T(8,128)(2,1)S(1)} %add_add_fusion), channel_id=1, source_target_pairs={{0,64},{16,80},{32,96},{48,112},{64,0},{80,16},{96,32},{112,48},{1... | collective-permute-start | bytes 1572872 | tf_op jit(solution)/shard_map/ppermute | solution.py:139
